TPU v7x, 256 devices: a whole 4x4x8 slice. The times are simulated.
256 devices in a mesh: pts: 32 (over x, y, core), wid: 8 (over z).
Axes of the slice: x: 4, y: 4, z: 8, core: 2. Of those that a mesh axis runs over, the one named last changes fastest.
Arguments:
- vertex_features: bfloat16 [360448, 512], P('pts'), may hold values from -40 to 40, as said below
- entry_matrix: bfloat16 [512, 512], P(None, 'wid'), may hold values from -2 to 2, as said below
- partition_matrix: bfloat16 [64, 32], replicated, may hold values from -3 to 3, as said below
- sharpness_matrix: float32 [64], replicated, may hold values from -3 to 3, as said below
- summary_qkv_matrix: float32 [3, 64, 64], replicated, may hold values from -3 to 3
- exit_matrix: bfloat16 [512, 512], P('wid'), may hold values from -0.5 to 0.5
- widening_matrix: bfloat16 [512, 512], P('wid'), may hold values from -0.25 to 0.25
- narrowing_matrix: bfloat16 [512, 512], P('wid'), may hold values from -0.25 to 0.25
Outputs:
- result: bfloat16 [360448, 512], P(('pts', 'wid'))
Inputs may be any that keep to these rules, and one draw needn't show every extreme that they name: `vertex_features`: features of the points, of order one to ten. `entry_matrix`: weights of the point projection. `partition_matrix`: slice logit weights. `sharpness_matrix`: temperature weights.
All inputs are finite; a program needn't handle non-finite values.
Results may differ from a plain program's by a relative error of at most 0.013.
Values may be sent and summed in bfloat16 or wider, within the bound.
A program may use at most 128 MiB of HBM per device.

v0:
```python
import jax
import jax.numpy as jnp
from jax import lax
from jax.sharding import PartitionSpec as P


def sent_to_all(array, axis):
    copies = jnp.broadcast_to(array, (lax.axis_size(axis), *array.shape))
    return lax.all_to_all(copies, axis, split_axis=0, concat_axis=0, tiled=True)


def of_everyone(array, axis):
    return sent_to_all(array, axis).sum(axis=0)


def in_one(arrays, axis):
    vector, at, outs = (jnp.concatenate([a.reshape(-1) for a in arrays]), 0, [])
    running = of_everyone(vector, axis)
    for a in arrays:
        outs.append(running[at : at + a.size].reshape(a.shape))
        at += a.size
    return tuple(outs)


def in_one_piece(arrays, axis, dim, along):
    both = jnp.concatenate(arrays, axis=along)
    out, at, outs = (lax.all_gather(both, axis, axis=dim, tiled=True), 0, [])
    for a in arrays:
        outs.append(lax.slice_in_dim(out, at, at + a.shape[along], axis=along))
        at += a.shape[along]
    return tuple(outs)


def layer_norm(values):
    centred = values - jnp.mean(values, axis=-1, keepdims=True)
    variance = jnp.mean(centred * centred, axis=-1, keepdims=True)
    return centred * lax.rsqrt(variance + 1e-05)


def project_tokens(token_rows, summary_qkv_matrix):
    highest = lax.Precision.HIGHEST
    queries = jnp.einsum("hgd,de->hge", token_rows, summary_qkv_matrix[0], precision=highest)
    keys_all = jnp.einsum("hgd,de->hge", token_rows, summary_qkv_matrix[1], precision=highest)
    value_rows_total = jnp.einsum(
        "hgd,de->hge", token_rows, summary_qkv_matrix[2], precision=highest
    )
    return (queries, keys_all, value_rows_total)


def local(
    vertex_features,
    entry_matrix,
    partition_matrix,
    sharpness_matrix,
    summary_qkv_matrix,
    exit_matrix,
    widening_matrix,
    narrowing_matrix,
):
    head_size = summary_qkv_matrix.shape[1]
    point_rows = vertex_features.shape[0]
    wid_count = lax.axis_size("wid")
    row_block = point_rows // wid_count
    features = vertex_features.astype(jnp.float32)
    normed = layer_norm(features).astype(jnp.bfloat16)
    feats = jnp.dot(normed, entry_matrix, preferred_element_type=jnp.float32).astype(jnp.bfloat16)
    local_heads = feats.shape[1] // head_size
    attention_cluster = feats.reshape(point_rows, local_heads, head_size)
    partition_sharpness = 0.5 + jax.nn.softplus(
        jnp.einsum(
            "kgv,v->kg", attention_cluster, sharpness_matrix, preferred_element_type=jnp.float32
        )
    )
    partition_scores = jnp.einsum(
        "nhd,dg->nhg", attention_cluster, partition_matrix, preferred_element_type=jnp.float32
    )
    partition_mapping = jax.nn.softmax(
        partition_scores / partition_sharpness[:, :, None], axis=-1
    ).astype(jnp.bfloat16)
    numerator = jnp.einsum(
        "nhg,nhd->hgd", partition_mapping, attention_cluster, preferred_element_type=jnp.float32
    )
    mass = jnp.sum(partition_mapping, axis=0, dtype=jnp.float32)
    numerator, mass = in_one((numerator, mass), "pts")
    token_rows = numerator / (mass[:, :, None] + 1e-05)
    queries, keys_all, value_rows_total = project_tokens(token_rows, summary_qkv_matrix)
    highest = lax.Precision.HIGHEST
    scores = jnp.einsum("hge,hke->hgk", queries, keys_all, precision=highest) / jnp.sqrt(
        jnp.float32(head_size)
    )
    attend = jax.nn.softmax(scores, axis=-1)
    out_tok = jnp.einsum("hgk,hke->hge", attend, value_rows_total, precision=highest).astype(
        jnp.bfloat16
    )
    deslice = jnp.einsum(
        "nhg,hgd->nhd", partition_mapping, out_tok, preferred_element_type=jnp.float32
    ).astype(jnp.bfloat16)
    deslice = deslice.reshape(point_rows, local_heads * head_size)
    mixed_rows = lax.all_to_all(deslice, "wid", split_axis=0, concat_axis=1, tiled=True)
    out_full, up_full, down_full = in_one_piece(
        (exit_matrix, widening_matrix, narrowing_matrix), "wid", 0, 1
    )
    attn_rows = jnp.dot(mixed_rows, out_full, preferred_element_type=jnp.float32)
    own_rows = lax.dynamic_slice_in_dim(features, lax.axis_index("wid") * row_block, row_block, 0)
    midway = own_rows + attn_rows
    normed2 = layer_norm(midway).astype(jnp.bfloat16)
    hidden = jax.nn.gelu(jnp.dot(normed2, up_full, preferred_element_type=jnp.float32)).astype(
        jnp.bfloat16
    )
    return (midway + jnp.dot(hidden, down_full, preferred_element_type=jnp.float32)).astype(
        jnp.bfloat16
    )


def solution(mesh):
    placed = (
        P("pts", None),
        P(None, "wid"),
        P(),
        P(),
        P(),
        P("wid", None),
        P("wid", None),
        P("wid", None),
    )
    return jax.shard_map(
        local, mesh=mesh, in_specs=placed, out_specs=P(("pts", "wid"), None), check_vma=False
    )
```

profile of v0, /device:TPU:1, one launch (start us, length us, event | category | flops | bytes accessed | tf_op | source)
XLA Modules:
  0.0 142.0 jit_solution(1057841601205365358)
XLA Ops:
  6.5 0.0 copy-start
  6.5 14.9 %copy.20 = bf16[11264,512]{0,1:T(8,128)(2,1)} copy(bf16[11264,512]{1,0:T(8,128)(2,1)} %param.8) | data formatting | bytes 23068672 | tf_op args[0]
  21.4 7.2 %convert_reduce_fusion = f32[11264]{0:T(1024)S(1)} fusion(bf16[11264,512]{0,1:T(8,128)(2,1)} %copy.20), kind=kLoop, calls=%fused_computation.2 | loop fusion | flops 11523072 | bytes 11579392 | tf_op jit(solution)/shard_map/reduce_sum | solution.py:35
  28.6 7.4 %multiply_reduce_fusion = f32[11264]{0:T(1024)S(1)} fusion(bf16[11264,512]{0,1:T(8,128)(2,1)} %copy.20, f32[11264]{0:T(1024)S(1)} %broadcast_multiply_fusion), kind=kLoop, calls=%fused_computation.1 | loop fusion | flops 23057408 | bytes 11624448 | tf_op jit(solution)/shard_map/reduce_sum | solution.py:36
  36.0 0.0 copy-done
  36.0 0.0 copy-start.6
  36.0 0.0 copy-start.7
  36.0 7.6 %convolution_convert_fusion = bf16[11264,64]{0,1:T(8,128)(2,1)S(1)} fusion(bf16[512,64]{0,1:T(8,128)(2,1)S(1)} %copy-done, bf16[11264,512]{0,1:T(8,128)(2,1)} %copy.20, f32[11264]{0:T(1024)S(1)} %add_rsqrt_fusion, f32[11264]{0:T(1024)S(1)} %broadcast_multiply_fusion), kind=kOutput, calls=%fused_computation.3 | convolution fusion | flops 761987072 | bytes 13131776 | tf_op jit(solution)/shard_map/dot_general | solution.py:66
  43.6 0.0 copy-done.6
  43.6 0.3 fusion.43
  44.0 0.0 copy-done.7
  44.0 0.4 fusion.40
  44.4 0.3 fusion.14
  44.7 0.0 copy-start.3
  44.7 0.0 copy-start.4
  44.7 0.0 copy-start.5
  44.7 0.0 copy-start.2
  44.8 0.4 convert_reduce_fusion.1
  45.1 0.5 fusion.46
  45.6 0.1 reshape.171
  45.7 0.9 broadcast_in_dim.2
  46.6 8.6 %all-to-all-start = ((f32[32,1,2080]{2,1,0:T(1,128)}), f32[32,1,2080]{2,1,0:T(1,128)S(1)}, u32[]{:S(2)}, u32[]{:S(2)}) async-start(f32[32,1,2080]{2,1,0:T(1,128)} %broadcast_in_dim.2), calls=%async_computation | async-start | bytes 557056 | tf_op jit(solution)/shard_map/all_to_all | solution.py:9
  55.2 0.2 all-gather.2.cloned.1.call-start
  55.4 0.0 copy-done.3
  55.4 0.0 copy-done.4
  55.4 0.0 copy-done.5
  55.4 0.7 pad_maximum_fusion
  56.1 0.0 all-gather.2.cloned.1.call-update
  56.2 8.1 %all-to-all-done = f32[32,1,2080]{2,1,0:T(1,128)S(1)} async-done(((f32[32,1,2080]{2,1,0:T(1,128)}), f32[32,1,2080]{2,1,0:T(1,128)S(1)}, u32[]{:S(2)}, u32[]{:S(2)}) %all-to-all-start) | async-done | bytes 266272 | tf_op jit(solution)/shard_map/all_to_all | solution.py:9
  64.3 0.2 reduce_sum.76
  64.5 0.1 broadcast_reduce_fusion
  64.6 0.1 div.84
  64.7 0.1 div.86
  64.8 0.0 copy-done.2
  64.8 0.1 fusion.22
  64.9 0.1 fusion.24
  65.1 0.1 fusion.20
  65.2 0.2 fusion.41
  65.4 0.2 convolution_convert_fusion.2
  65.7 0.6 convolution_convert_fusion.1
  66.2 0.2 copy.29
  66.4 1.3 copy.22
  67.7 8.2 %all-to-all-start.1 = ((bf16[8,1408,64]{1,2,0:T(8,128)(2,1)}), bf16[8,1408,64]{1,2,0:T(8,128)(2,1)S(1)}, u32[]{:S(2)}, u32[]{:S(2)}) async-start(bf16[8,1408,64]{1,2,0:T(8,128)(2,1)} %copy.22), calls=%async_computation.1 | async-start | bytes 2883584 | tf_op jit(solution)/shard_map/all_to_all | solution.py:99
  75.9 13.0 %convert_element_type.39 = f32[11264,512]{0,1:T(8,128)} convert(bf16[11264,512]{0,1:T(8,128)(2,1)} %copy.20) | non-fusion elementwise | flops 5767168 | bytes 34603008 | tf_op jit(solution)/shard_map/convert_element_type | solution.py:64
  88.9 29.2 %all-gather.2.cloned.1.call-done = bf16[512,1536]{1,0:T(8,128)(2,1)} async-done(((bf16[64,1536]{1,0:T(8,128)(2,1)}), bf16[512,1536]{1,0:T(8,128)(2,1)}) %all-gather.2.cloned.1.call-update) | async-done | bytes 1572880 | tf_op jit(solution)/shard_map/all_gather | solution.py:27
  118.1 5.1 %all-to-all-done.1 = bf16[8,1408,64]{1,2,0:T(8,128)(2,1)S(1)} async-done(((bf16[8,1408,64]{1,2,0:T(8,128)(2,1)}), bf16[8,1408,64]{1,2,0:T(8,128)(2,1)S(1)}, u32[]{:S(2)}, u32[]{:S(2)}) %all-to-all-start.1) | async-done | bytes 1441824 | tf_op jit(solution)/shard_map/all_to_all | solution.py:99
  123.1 0.0 copy-start.1
  123.1 1.1 copy-done.1
  124.2 3.5 %fusion.42 = (f32[1408]{0:T(1024)S(1)}, f32[1408,512]{0,1:T(8,128)S(1)}) fusion(bf16[1408,512]{0,1:T(8,128)(2,1)} %bitcast.48, bf16[512,1536]{1,0:T(8,128)(2,1)} %all-gather.2.cloned.1.call-done, f32[11264,512]{0,1:T(8,128)} %convert_element_type.39, s32[]{:T(128)S(6)} %select_n.8), kind=kOutput, calls=%fused_computation.67 | convolution fusion | flops 739637888 | bytes 7738884 | tf_op jit(solution)/shard_map/dot_general | solution.py:103
  127.7 0.3 multiply_reduce_fusion.1
  128.0 4.6 %fusion.2 = bf16[1408,512]{0,1:T(8,128)(2,1)} fusion(f32[1408,512]{0,1:T(8,128)S(1)} %get-tuple-element.12, f32[1408]{0:T(1024)S(1)} %add_rsqrt_fusion.1, f32[1408]{0:T(1024)S(1)} %broadcast_multiply_fusion.1, bf16[512,1536]{1,0:T(8,128)(2,1)} %all-gather.2.cloned.1.call-done), kind=kOutput, calls=%fused_computation.11 | convolution fusion | flops 1486487552 | bytes 8273920 | tf_op jit(solution)/shard_map/dot_general | solution.py:110
  132.6 2.5 %copy.24 = bf16[1408,512]{1,0:T(8,128)(2,1)} copy(bf16[1408,512]{0,1:T(8,128)(2,1)} %fusion.2) | data formatting | bytes 2883584 | tf_op jit(solution)/shard_map/convert_element_type | solution.py:110
  (9 shorter events, 0.1 us)
Async XLA Ops:
  6.5 29.5 %copy-start = (bf16[512,64]{0,1:T(8,128)(2,1)S(1)}, bf16[512,64]{0,1:T(8,128)(2,1)}, u32[]{:S(2)}) copy-start(bf16[512,64]{0,1:T(8,128)(2,1)} %param.9) | copy-start | bytes 196612
  36.0 7.6 %copy-start.6 = (f32[64]{0:T(128)S(1)}, f32[64]{0:T(128)}, u32[]{:S(2)}) copy-start(f32[64]{0:T(128)} %param.11) | copy-start | bytes 772
  36.0 8.0 %copy-start.7 = (bf16[64,32]{0,1:T(8,128)(2,1)S(1)}, bf16[64,32]{0,1:T(8,128)(2,1)}, u32[]{:S(2)}) copy-start(bf16[64,32]{0,1:T(8,128)(2,1)} %param.10) | copy-start | bytes 12292
  44.7 10.7 %copy-start.3 = (bf16[64,512]{1,0:T(8,128)(2,1)S(1)}, bf16[64,512]{1,0:T(8,128)(2,1)}, u32[]{:S(2)}) copy-start(bf16[64,512]{1,0:T(8,128)(2,1)} %param.15) | copy-start | bytes 196612
  44.7 10.7 %copy-start.4 = (bf16[64,512]{1,0:T(8,128)(2,1)S(1)}, bf16[64,512]{1,0:T(8,128)(2,1)}, u32[]{:S(2)}) copy-start(bf16[64,512]{1,0:T(8,128)(2,1)} %param.14) | copy-start | bytes 196612
  44.7 10.7 %copy-start.5 = (bf16[64,512]{1,0:T(8,128)(2,1)S(1)}, bf16[64,512]{1,0:T(8,128)(2,1)}, u32[]{:S(2)}) copy-start(bf16[64,512]{1,0:T(8,128)(2,1)} %param.13) | copy-start | bytes 196612
  44.7 20.0 %copy-start.2 = (f32[3,64,64]{2,1,0:T(8,128)S(1)}, f32[3,64,64]{2,1,0:T(8,128)}, u32[]{:S(2)}) copy-start(f32[3,64,64]{2,1,0:T(8,128)} %param.12) | copy-start | bytes 147460
  46.6 17.7 %all-to-all-start = ((f32[32,1,2080]{2,1,0:T(1,128)}), f32[32,1,2080]{2,1,0:T(1,128)S(1)}, u32[]{:S(2)}, u32[]{:S(2)}) async-start(f32[32,1,2080]{2,1,0:T(1,128)} %broadcast_in_dim.2), calls=%async_computation | async-start | bytes 557056 | tf_op jit(solution)/shard_map/all_to_all | solution.py:9
  55.2 62.9 %all-gather.2.cloned.1.call-start = ((), (), s32[]{:S(2)}) async-start(), calls=%async_computation.2 | async-start | bytes 1769472 | tf_op jit(solution)/shard_map/all_gather | solution.py:27
  67.7 55.5 %all-to-all-start.1 = ((bf16[8,1408,64]{1,2,0:T(8,128)(2,1)}), bf16[8,1408,64]{1,2,0:T(8,128)(2,1)S(1)}, u32[]{:S(2)}, u32[]{:S(2)}) async-start(bf16[8,1408,64]{1,2,0:T(8,128)(2,1)} %copy.22), calls=%async_computation.1 | async-start | bytes 2883584 | tf_op jit(solution)/shard_map/all_to_all | solution.py:99
  123.1 1.1 copy-start.1
Sparse Core Ops, SparseCore 0:
  57.8 60.2 all-gather.1
where the time goes:
time: 143 us; the launch traced here: 142 us
  waiting for transfers between devices  42.4 us (30%)
  other arithmetic  29.5 us (21%)
  local copies, waits for them, and re-layouts  21.2 us (15%)
  matrix products  18.2 us (13%)
  starting transfers between devices  17 us (12%)
  between operations  13.6 us (10%)
    all_gather x1, waiting for transfers between devices, in_one_piece(): out, at, outs = (lax.all_gather(both, axis, axis=dim, tiled=True), 0, [])  29.2 us
    unnamed x18, local copies, waits for them, and re-layouts  16.2 us
    convert_element_type x1, other arithmetic, local(): features = vertex_features.astype(jnp.float32)  13 us
    all_to_all x1, starting transfers between devices, sent_to_all(): return lax.all_to_all(copies, axis, split_axis=0, concat_axis=0, tiled=True)  8.58 us
    all_to_all x1, starting transfers between devices, local(): lax.all_to_all(deslice, 'wid', split_axis=0, concat_axis=1, tiled=True)  8.18 us
    all_to_all x1, waiting for transfers between devices, sent_to_all(): return lax.all_to_all(copies, axis, split_axis=0, concat_axis=0, tiled=True)  8.14 us
    reduce_sum x2, other arithmetic, layer_norm(): variance = jnp.mean(centred * centred, axis=-1, keepdims=True)  7.73 us
    dot_general x1, matrix products, local(): jnp.dot(normed, entry_matrix, preferred_element_type=jnp.float32)  7.6 us
  transfers between devices with their start and end apart: 3, of which 3 were waited for; matrix products, arithmetic and copies ran while one was open for 12% of the time, Pallas kernels for 0%

commit v1 on v0

v1 whole, which is shorter than its diff:
```python
import functools

import jax
import jax.numpy as jnp
from jax import lax
from jax.experimental import pallas as pl
from jax.experimental.pallas import tpu as pltpu
from jax.sharding import PartitionSpec as P

MESH = pl.DeviceIdType.MESH
F32, BF16 = jnp.float32, jnp.bfloat16
HIGH = lax.Precision.HIGHEST

D, H, DH, G = 512, 8, 64, 32
ROWS = 11264
OWN = 1408
BLK = 1024
NBLK = ROWS // BLK
TBLK = 352
HALF = DH // 2

X_PEERS = [(dx, dc) for dx in range(4) for dc in range(2)]


def contract_lanes(a, b, precision=None):
    return lax.dot_general(
        a, b, (((1,), (1,)), ((), ())), preferred_element_type=F32, precision=precision
    )


def softmax_weights(logits, temperature_logit):
    soft = jnp.maximum(temperature_logit, 0.0) + jnp.log(1.0 + jnp.exp(-jnp.abs(temperature_logit)))
    scaled = logits * (1.0 / (0.5 + soft))
    e = jnp.exp(scaled - jnp.max(scaled, axis=0, keepdims=True))
    return (e * (1.0 / jnp.sum(e, axis=0, keepdims=True))).astype(BF16)


def kernel(
    x_hbm, entry_hbm, part_ref, sharp_ref, qkv_ref, exit_hbm, wide_hbm, narrow_hbm,
    out_hbm,
    xv, eh, waug, pT, cs, mu_s, rs_s, yT0, yT1, acc, wall, yall, wT, wn, mbuf, outv,
    xbuf, ybuf, zbuf,
    x_sem, in_sem, out_sem,
    ring_send, ring_recv, d2d_send, d2d_recv,
    xs_send, xs_recv, ys_send, ys_recv, zs_send, zs_recv,
):
    pts, z = lax.axis_index("pts"), lax.axis_index("wid")
    core = lax.rem(pts, 2)
    gx, gy = pts // 8, lax.rem(pts // 2, 4)
    partner = pts + 1 - 2 * core

    def pts_at(dx, dy, dc):
        return (lax.rem(gx + dx, 4) * 4 + lax.rem(gy + dy, 4)) * 2 + lax.rem(core + dc, 2)

    def z_at(dz):
        return lax.rem(z + dz + H, H)

    def x_copy(i):
        return pltpu.make_async_copy(
            x_hbm.at[pl.ds(i * BLK, BLK)], xv.at[pl.ds(i * BLK, BLK)], x_sem.at[i]
        )

    entry_copy = pltpu.make_async_copy(entry_hbm, eh, in_sem.at[0])
    entry_copy.start()
    for i in range(NBLK):
        x_copy(i).start()
    own_copies = []
    for k, ref in ((1, exit_hbm), (2, wide_hbm), (3, narrow_hbm)):
        for c in range(2):
            own_copies.append(
                pltpu.make_async_copy(
                    ref.at[pl.ds(c * HALF, HALF)], wall.at[k, z, c], in_sem.at[2 * k - 1 + c]
                )
            )
    for copy in own_copies:
        copy.start()

    barrier = pltpu.get_barrier_semaphore()
    for dx, dc in X_PEERS[1:]:
        pl.semaphore_signal(barrier, inc=1, device_id=(pts_at(dx, 0, dc), z), device_id_type=MESH)
    for dy in range(1, 4):
        pl.semaphore_signal(barrier, inc=1, device_id=(pts_at(0, dy, 0), z), device_id_type=MESH)
    for dz in range(1, H):
        pl.semaphore_signal(barrier, inc=1, device_id=(pts, z_at(dz)), device_id_type=MESH)

    partT = part_ref[...].astype(F32).T.astype(BF16)
    sharp = jnp.broadcast_to(sharp_ref[...], (16, DH))
    sharp_hi = sharp.astype(BF16).astype(F32)
    row16 = lax.broadcasted_iota(jnp.int32, (16, DH), 0)
    tail = jnp.where(row16 == 0, sharp_hi, jnp.where(row16 == 1, sharp - sharp_hi, 0.0))
    pT[0:G, :] = partT
    pT[G : G + 16, :] = tail.astype(BF16)

    entry_copy.wait()
    ehT = eh[...].astype(F32).T
    ehT_bf = ehT.astype(BF16)
    wall[0, z] = ehT_bf.reshape(2, HALF, D)
    cs[...] = jnp.broadcast_to(jnp.sum(ehT, axis=1, keepdims=True), (DH, 128))
    rowd = lax.broadcasted_iota(jnp.int32, (DH, D), 0)
    waug[...] = jnp.concatenate([ehT, jnp.where(rowd == 0, 1.0 / D, 0.0)], axis=0).T.astype(BF16)
    acc[...] = jnp.zeros_like(acc)
    ones16 = jnp.ones((16, BLK), BF16)

    def part_of(g, shard, half, d, s):
        rows = pl.ds(0, HALF) if s < 4 else (pl.ds(0, HALF // 2) if d > 0 else pl.ds(HALF // 2, HALF // 2))
        mats = pl.ds(0, 1) if g == 0 else pl.ds(1, 3)
        return wall.at[mats, shard, half, rows]

    def ring(g, d, s):
        ref = part_of(g, z_at(-d * (s - 1)), core, d, s)
        at = (g, (1 - d) // 2, s - 1)
        return pltpu.make_async_remote_copy(
            src_ref=ref, dst_ref=ref, send_sem=ring_send.at[at], recv_sem=ring_recv.at[at],
            device_id=(pts, z_at(d)), device_id_type=MESH,
        )

    def arrival(g, d, s):
        ref = part_of(g, z_at(-d * s), core, d, s)
        at = (g, (1 - d) // 2, s - 1)
        return pltpu.make_async_remote_copy(
            src_ref=ref, dst_ref=ref, send_sem=ring_send.at[at], recv_sem=ring_recv.at[at],
            device_id=(pts, z_at(d)), device_id_type=MESH,
        )

    def to_partner(g, d, s):
        ref = part_of(g, z_at(-d * s), core, d, s)
        at = (g, (1 - d) // 2, s - 1)
        return pltpu.make_async_remote_copy(
            src_ref=ref, dst_ref=ref, send_sem=d2d_send.at[at], recv_sem=d2d_recv.at[at],
            device_id=(partner, z), device_id_type=MESH,
        )

    def from_partner(g, d, s):
        ref = part_of(g, z_at(-d * s), 1 - core, d, s)
        at = (g, (1 - d) // 2, s - 1)
        return pltpu.make_async_remote_copy(
            src_ref=ref, dst_ref=ref, send_sem=d2d_send.at[at], recv_sem=d2d_recv.at[at],
            device_id=(partner, z), device_id_type=MESH,
        )

    def ring_start():
        for copy in own_copies:
            copy.wait()
        pl.semaphore_wait(barrier, 7 + 3 + 7)
        for g in range(2):
            for d in (1, -1):
                ring(g, d, 1).start()

    def ring_step(g, s):
        for d in (1, -1):
            arrival(g, d, s).wait_recv()
            if s < 4:
                ring(g, d, s + 1).start()
            to_partner(g, d, s).start()

    def project(i, yT):
        x_copy(i).wait()
        xb = xv[pl.ds(pl.multiple_of(i * BLK, BLK), BLK), :]
        y = jnp.dot(xb, waug[...], preferred_element_type=F32)
        xf = xb.astype(F32)
        sq = xf * xf
        sq = (sq[:, 0:128] + sq[:, 128:256]) + (sq[:, 256:384] + sq[:, 384:512])
        total = jnp.sum(sq, axis=1, keepdims=True)
        lane = lax.broadcasted_iota(jnp.int32, (BLK, 128), 1)
        yT[...] = jnp.where(lane == DH + 1, total, y).T

    def slices(i, yT):
        mean = yT[DH : DH + 1, :]
        var = jnp.maximum(yT[DH + 1 : DH + 2, :] * (1.0 / D) - mean * mean, 0.0)
        rstd = lax.rsqrt(var + 1e-05)
        lanes = pl.ds(pl.multiple_of(i * BLK, BLK), BLK)
        mu_s[:, lanes] = mean
        rs_s[:, lanes] = rstd
        feats = ((yT[0:DH, :] - cs[:, 0:1] * mean) * rstd).astype(BF16)
        logits = jnp.dot(pT[...], feats, preferred_element_type=F32)
        w = softmax_weights(logits[0:G], logits[G : G + 1] + logits[G + 1 : G + 2])
        acc[...] += contract_lanes(jnp.concatenate([feats, ones16], axis=0), w)

    project(0, yT0)

    def two_blocks(j, _):
        @pl.when(j == 2)
        def _():
            ring_start()

        @pl.when(j == 4)
        def _():
            ring_step(0, 1)

        slices(2 * j, yT0)
        project(2 * j + 1, yT1)
        slices(2 * j + 1, yT1)
        project(2 * j + 2, yT0)
        return 0

    lax.fori_loop(0, NBLK // 2, two_blocks, 0)
    slices(NBLK - 1, yT0)

    xbuf[0] = jnp.concatenate([acc[...], jnp.zeros((48, G), F32)], axis=0).T

    def x_send(r):
        dx, dc = X_PEERS[r]
        return pltpu.make_async_remote_copy(
            src_ref=xbuf.at[0], dst_ref=xbuf.at[r], send_sem=xs_send.at[r], recv_sem=xs_recv.at[r],
            device_id=(pts_at(dx, 0, dc), z), device_id_type=MESH,
        )

    def y_send(r):
        return pltpu.make_async_remote_copy(
            src_ref=ybuf.at[0], dst_ref=ybuf.at[r], send_sem=ys_send.at[r], recv_sem=ys_recv.at[r],
            device_id=(pts_at(0, r, 0), z), device_id_type=MESH,
        )

    for r in range(1, 8):
        x_send(r).start()
    ring_step(0, 2)
    ring_step(1, 1)
    ring_step(0, 3)
    for r in range(1, 8):
        x_send(r).wait_recv()
    ybuf[0] = jnp.sum(xbuf[...], axis=0)
    for r in range(1, 4):
        y_send(r).start()
    ring_step(1, 2)
    ring_step(0, 4)

    for s in range(1, 5):
        for d in (1, -1):
            from_partner(0, d, s).wait_recv()
    own = pl.multiple_of(z * OWN, 128)
    entryT = wall[0].reshape(D, D)
    yall[...] = contract_lanes(entryT, xv[pl.ds(own, OWN), :])
    colsum = jnp.sum(entryT.astype(F32), axis=1, keepdims=True)
    mean_own = mu_s[:, pl.ds(own, OWN)]
    yall[...] = (yall[...] - colsum * mean_own) * rs_s[:, pl.ds(own, OWN)]
    ring_step(1, 3)

    def own_head(h, _):
        feats = yall[pl.ds(pl.multiple_of(h * DH, DH), DH), :].astype(BF16)
        logits = jnp.dot(pT[...], feats, preferred_element_type=F32)
        w = softmax_weights(logits[0:G], logits[G : G + 1] + logits[G + 1 : G + 2])
        wT[pl.ds(pl.multiple_of(h * G, G), G), :] = w
        return 0

    lax.fori_loop(0, H, own_head, 0)
    wn[...] = wT[...].T

    for r in range(1, 4):
        y_send(r).wait_recv()
    sums = jnp.sum(ybuf[...], axis=0)
    tokens = sums[:, 0:DH] / (sums[:, DH : DH + 1] + 1e-05)
    queries = jnp.dot(tokens, qkv_ref[0], preferred_element_type=F32, precision=HIGH)
    keys = jnp.dot(tokens, qkv_ref[1], preferred_element_type=F32, precision=HIGH)
    values = jnp.dot(
        tokens, jnp.concatenate([qkv_ref[2], jnp.zeros((DH, DH), F32)], axis=1),
        preferred_element_type=F32, precision=HIGH,
    )
    scores = contract_lanes(queries, keys, precision=HIGH) * 0.125
    e = jnp.exp(scores - jnp.max(scores, axis=1, keepdims=True))
    attend = e / jnp.sum(e, axis=1, keepdims=True)
    zbuf[z] = jnp.dot(attend, values, preferred_element_type=F32, precision=HIGH).astype(BF16)

    def z_send(dz):
        return pltpu.make_async_remote_copy(
            src_ref=zbuf.at[z], dst_ref=zbuf.at[z], send_sem=zs_send.at[dz], recv_sem=zs_recv.at[dz],
            device_id=(pts, z_at(dz)), device_id_type=MESH,
        )

    def z_arrival(dz):
        at = zbuf.at[z_at(-dz)]
        return pltpu.make_async_remote_copy(
            src_ref=at, dst_ref=at, send_sem=zs_send.at[dz], recv_sem=zs_recv.at[dz],
            device_id=(pts, z_at(dz)), device_id_type=MESH,
        )

    for dz in range(1, H):
        z_send(dz).start()
    ring_step(1, 4)
    for s in range(1, 5):
        for d in (1, -1):
            from_partner(1, d, s).wait_recv()
    for dz in range(1, H):
        z_arrival(dz).wait_recv()

    for h in range(H):
        mbuf[h * G : (h + 1) * G, :] = jnp.dot(
            zbuf[h][:, 0:DH], wall[1, h].reshape(DH, D), preferred_element_type=F32
        ).astype(BF16)

    def out_copy(t):
        rows = pl.ds(t * TBLK, TBLK)
        return pltpu.make_async_copy(outv.at[rows], out_hbm.at[rows], out_sem.at[t])

    def tail_rows(t, _):
        rows = pl.ds(pl.multiple_of(t * TBLK, 32), TBLK)
        x_rows = xv[pl.ds(pl.multiple_of(own + t * TBLK, 32), TBLK), :].astype(F32)
        midway = x_rows + jnp.dot(wn[rows, :], mbuf[...], preferred_element_type=F32)
        centred = midway - jnp.mean(midway, axis=1, keepdims=True)
        var = jnp.mean(centred * centred, axis=1, keepdims=True)
        normed = (centred * lax.rsqrt(var + 1e-05)).astype(BF16)
        hidden = jnp.dot(normed, wall[2].reshape(D, D), preferred_element_type=F32)
        hidden = jax.nn.gelu(hidden).astype(BF16)
        out = midway + jnp.dot(hidden, wall[3].reshape(D, D), preferred_element_type=F32)
        outv[rows, :] = out.astype(BF16)
        out_copy(t).start()
        return 0

    lax.fori_loop(0, OWN // TBLK, tail_rows, 0)

    for g in range(2):
        for d in (1, -1):
            for s in range(1, 5):
                ring(g, d, s).wait_send()
                to_partner(g, d, s).wait_send()
    for r in range(1, 8):
        x_send(r).wait_send()
    for r in range(1, 4):
        y_send(r).wait_send()
    for dz in range(1, H):
        z_send(dz).wait_send()
    for t in range(OWN // TBLK):
        out_copy(t).wait()


def local(x, entry, partition, sharpness, qkv, exit_matrix, widening, narrowing):
    hbm = pl.BlockSpec(memory_space=pl.ANY)
    vmem = pl.BlockSpec(memory_space=pltpu.VMEM)
    dma = pltpu.SemaphoreType.DMA
    return pl.pallas_call(
        kernel,
        out_shape=jax.ShapeDtypeStruct((OWN, D), BF16),
        in_specs=[hbm, hbm, vmem, vmem, vmem, hbm, hbm, hbm],
        out_specs=hbm,
        scratch_shapes=[
            pltpu.VMEM((ROWS, D), BF16),
            pltpu.VMEM((D, DH), BF16),
            pltpu.VMEM((D, 128), BF16),
            pltpu.VMEM((G + 16, DH), BF16),
            pltpu.VMEM((DH, 128), F32),
            pltpu.VMEM((1, ROWS), F32),
            pltpu.VMEM((1, ROWS), F32),
            pltpu.VMEM((128, BLK), F32),
            pltpu.VMEM((128, BLK), F32),
            pltpu.VMEM((DH + 16, G), F32),
            pltpu.VMEM((4, H, 2, HALF, D), BF16),
            pltpu.VMEM((D, OWN), F32),
            pltpu.VMEM((H * G, OWN), BF16),
            pltpu.VMEM((OWN, H * G), BF16),
            pltpu.VMEM((H * G, D), BF16),
            pltpu.VMEM((OWN, D), BF16),
            pltpu.VMEM((8, G, 128), F32),
            pltpu.VMEM((4, G, 128), F32),
            pltpu.VMEM((H, G, 128), BF16),
            dma((NBLK,)),
            dma((8,)),
            dma((OWN // TBLK,)),
            dma((2, 2, 4)),
            dma((2, 2, 4)),
            dma((2, 2, 4)),
            dma((2, 2, 4)),
            dma((8,)),
            dma((8,)),
            dma((4,)),
            dma((4,)),
            dma((8,)),
            dma((8,)),
        ],
        compiler_params=pltpu.CompilerParams(
            collective_id=0, has_side_effects=True, vmem_limit_bytes=60 * 2**20
        ),
    )(x, entry, partition, sharpness.reshape(1, DH), qkv, exit_matrix, widening, narrowing)


def solution(mesh):
    placed = (
        P("pts", None), P(None, "wid"), P(), P(), P(),
        P("wid", None), P("wid", None), P("wid", None),
    )
    return jax.shard_map(
        local, mesh=mesh, in_specs=placed, out_specs=P(("pts", "wid"), None), check_vma=False
    )
```

time: 143 us -> 50 us (0.35)
  Pallas kernels: 0 us -> 43.9 us
  waiting for transfers between devices: 42.4 us -> 0 us
  other arithmetic: 29.5 us -> 0 us
  matrix products: 18.2 us -> 0 us
  starting transfers between devices: 17 us -> 0 us
  local copies, waits for them, and re-layouts: 21.2 us -> 5.53 us
  between operations: 13.6 us -> 0.01 us
    pallas_call x0 -> x1, Pallas kernels: none -> 43.9 us  [local(): pl.pallas_call(kernel, out_shape=jax.ShapeDtypeStruct((OWN, D), BF16), in...]
    all_gather x1 -> x0, waiting for transfers between devices: 29.2 us -> none  [in_one_piece(): out, at, outs = (lax.all_gather(both, axis, axis=dim, tiled=True), 0, [])]
    dot_general x12 -> x0, matrix products: 18.2 us -> none  [the longest x1 7.6 us: local(): jnp.dot(normed, entry_matrix, preferred_element_type=jnp.float32)]
    all_to_all x2 -> x0, starting transfers between devices: 16.8 us -> none  [the longest x1 8.58 us: sent_to_all(): return lax.all_to_all(copies, axis, split_axis=0, concat_axis=0, tiled=True)]
    reduce_sum x7 -> x0, other arithmetic: 15.8 us -> none  [the longest x2 7.73 us: layer_norm(): variance = jnp.mean(centred * centred, axis=-1, keepdims=True)]
    all_to_all x2 -> x0, waiting for transfers between devices: 13.2 us -> none  [the longest x1 8.14 us: sent_to_all(): return lax.all_to_all(copies, axis, split_axis=0, concat_axis=0, tiled=True)]
    convert_element_type x1 -> x0, other arithmetic: 13 us -> none  [local(): features = vertex_features.astype(jnp.float32)]
    unnamed x18 -> x3, local copies, waits for them, and re-layouts: 16.2 us -> 5.53 us
  transfers between devices with their start and end apart: 3 -> 0, of which waited for: 3 -> 0; matrix products, arithmetic and copies ran while one was open for 12% -> 0% of each run, Pallas kernels for 0% -> 0%
where the time goes in v1:
time: 50 us; the launch traced here: 49.5 us
  Pallas kernels  43.9 us (88%)
  local copies, waits for them, and re-layouts  5.53 us (11%)
    pallas_call x1, Pallas kernels, local(): pl.pallas_call(kernel, out_shape=jax.ShapeDtypeStruct((OWN, D), BF16), in...  43.9 us
    unnamed x3, local copies, waits for them, and re-layouts  5.53 us

profile of v1, /device:TPU:1, one launch (start us, length us, event | category | flops | bytes accessed | tf_op | source)
XLA Modules:
  0.0 49.5 jit_solution(197595376359877272)
XLA Ops:
  0.0 1.4 %copy.10.part_ref = bf16[64,32]{1,0:T(8,128)(2,1)} copy(bf16[64,32]{0,1:T(8,128)(2,1)} %param.10) | data formatting | bytes 8192 | tf_op args[2]
  1.4 1.6 %copy.9.entry_hbm = bf16[512,64]{1,0:T(8,128)(2,1)} copy(bf16[512,64]{0,1:T(8,128)(2,1)} %param.9) | data formatting | bytes 131072 | tf_op args[1]
  3.0 43.9 %shard_map.82 = bf16[1408,512]{1,0:T(8,128)(2,1)} custom-call(bf16[11264,512]{1,0:T(8,128)(2,1)} %x_hbm.1, bf16[512,64]{1,0:T(8,128)(2,1)} %copy.9.entry_hbm, bf16[64,32]{1,0:T(8,128)(2,1)} %copy.10.part_ref, f32[1,64]{1,0:T(1,128)} %bitcast.1, f32[3,64,64]{2,1,0:T(8,128)} %qkv_ref.1, bf16[64,512]{1,0:T(8,128)(2,1)} %exit_hbm.1, bf16[64,512]{1,0:T(8,128)(2,1)} %wide_hbm.1, ...), custom_call_target="tpu_custom_call" | custom-call | tf_op jit(solution)/shard_map/pallas_call | solution.py:329
  46.9 2.6 %copy.12 = bf16[1408,512]{1,0:T(8,128)(2,1)} copy(bf16[1408,512]{1,0:T(8,128)(2,1)} %shard_map.82) | data formatting | bytes 2883584

commit v2 on v1

v2 whole, which is shorter than its diff:
```python
import functools

import jax
import jax.numpy as jnp
from jax import lax
from jax.experimental import pallas as pl
from jax.experimental.pallas import tpu as pltpu
from jax.sharding import PartitionSpec as P

MESH = pl.DeviceIdType.MESH
F32, BF16 = jnp.float32, jnp.bfloat16
HIGH = lax.Precision.HIGHEST

D, H, DH, G = 512, 8, 64, 32
ROWS = 11264
OWN = 1408
BLK = 1024
NBLK = ROWS // BLK
TBLK = 352
HALF = DH // 2

PLANE = [(dx, dy) for dx in range(4) for dy in range(4)]
Z_NEAR = (1, -1, 2, -2)
Z_FAR = ((-2, 1, (0, HALF)), (2, -1, (0, HALF)), (-2, 2, (0, HALF // 2)), (2, -2, (HALF // 2, HALF // 2)))


def contract_lanes(a, b, precision=None):
    return lax.dot_general(
        a, b, (((1,), (1,)), ((), ())), preferred_element_type=F32, precision=precision
    )


def softmax_weights(logits, temperature_logit):
    soft = jnp.maximum(temperature_logit, 0.0) + jnp.log(1.0 + jnp.exp(-jnp.abs(temperature_logit)))
    scaled = logits * (1.0 / (0.5 + soft))
    e = jnp.exp(scaled - jnp.max(scaled, axis=0, keepdims=True))
    return (e * (1.0 / jnp.sum(e, axis=0, keepdims=True))).astype(BF16)


def kernel(
    x_hbm, entry_hbm, part_ref, sharp_ref, qkv_ref, exit_hbm, wide_hbm, narrow_hbm,
    out_ref,
    xv, eh, waug, pT, cs, f0, f1, acc, wall, nown, wT, wn, mbuf, yall,
    pair, plane, zbuf,
    x_sem, in_sem, own_sem, far_sem, d2d_sem, pair_sem, plane_sem, z_sem,
):
    pts, z = lax.axis_index("pts"), lax.axis_index("wid")
    core = lax.rem(pts, 2)
    gx, gy = pts // 8, lax.rem(pts // 2, 4)
    partner = pts + 1 - 2 * core

    def pts_at(dx, dy):
        return (lax.rem(gx + dx, 4) * 4 + lax.rem(gy + dy, 4)) * 2 + core

    def z_at(dz):
        return lax.rem(z + dz + H, H)

    def x_copy(i):
        return pltpu.make_async_copy(
            x_hbm.at[pl.ds(i * BLK, BLK)], xv.at[pl.ds(i * BLK, BLK)], x_sem.at[i]
        )

    entry_copy = pltpu.make_async_copy(entry_hbm, eh, in_sem.at[0])
    entry_copy.start()
    x_copy(0).start()
    own_copies = []
    for k, ref in enumerate((entry_hbm, exit_hbm, wide_hbm, narrow_hbm)):
        for c in range(2):
            own_copies.append(
                pltpu.make_async_copy(
                    ref.at[pl.ds(c * HALF, HALF)], wall.at[k, z, c], in_sem.at[1 + 2 * k + c]
                )
            )

    barrier = pltpu.get_barrier_semaphore()
    pl.semaphore_signal(barrier, inc=1, device_id=(partner, z), device_id_type=MESH)
    for dx, dy in PLANE[1:]:
        pl.semaphore_signal(barrier, inc=1, device_id=(pts_at(dx, dy), z), device_id_type=MESH)
    for dz in range(1, H):
        pl.semaphore_signal(barrier, inc=1, device_id=(pts, z_at(dz)), device_id_type=MESH)

    sharp = jnp.broadcast_to(sharp_ref[...], (16, DH))
    sharp_hi = sharp.astype(BF16).astype(F32)
    row16 = lax.broadcasted_iota(jnp.int32, (16, DH), 0)
    tail = jnp.where(row16 == 0, sharp_hi, jnp.where(row16 == 1, sharp - sharp_hi, 0.0))
    table = jnp.concatenate([part_ref[...].astype(F32), tail], axis=0)
    pT[...] = jnp.concatenate([table, jnp.zeros((G + 16, DH), F32)], axis=1).astype(BF16)
    acc[...] = jnp.zeros_like(acc)
    one_at_64 = (lax.broadcasted_iota(jnp.int32, (1, 128), 1) == DH).astype(F32)

    entry_copy.wait()
    for i in range(1, NBLK):
        x_copy(i).start()
    for copy in own_copies:
        copy.start()
    head = jnp.concatenate([eh[...].astype(F32), jnp.zeros((DH, D), F32)], axis=0).T
    cs[...] = jnp.sum(head, axis=0, keepdims=True)
    waug[:, 0:128] = head.astype(BF16)
    waug[:, 128:256] = jnp.full((D, 128), 1.0 / D, BF16)

    mats = (pl.ds(0, 1), pl.ds(1, 3))

    def to(ref, sems, device, target=None):
        return pltpu.make_async_remote_copy(
            src_ref=ref, dst_ref=ref if target is None else target, send_sem=sems.at[0], recv_sem=sems.at[1],
            device_id=device, device_id_type=MESH,
        )

    def half_of(g, offset, half, rows=pl.ds(0, HALF)):
        return wall.at[mats[g], z_at(offset), half, rows]

    def of_size(g, n, sems):
        return to(wall.at[mats[g], pl.ds(0, n), 0], sems.at[g], (partner, z))

    def weights_start():
        for copy in own_copies:
            copy.wait()
        for g in range(2):
            for dz in Z_NEAR:
                to(half_of(g, 0, core), own_sem.at[g], (pts, z_at(dz))).start()

    def weights_onward(g):
        of_size(g, 4, own_sem).wait_recv()
        for source, dz, rows in Z_FAR:
            to(half_of(g, source, core, pl.ds(*rows)), far_sem.at[g], (pts, z_at(dz))).start()
        for offset in Z_NEAR:
            to(half_of(g, offset, core), d2d_sem.at[g], (partner, z)).start()

    def weights_far(g):
        of_size(g, 3, far_sem).wait_recv()
        for offset in (3, -3, 4):
            to(half_of(g, offset, core), d2d_sem.at[g], (partner, z)).start()

    def weights_done(g):
        of_size(g, 7, d2d_sem).wait_recv()

    def project(i, fbuf):
        x_copy(i).wait()
        xb = xv[pl.ds(pl.multiple_of(i * BLK, BLK), BLK), :]
        y = jnp.dot(xb, waug[...], preferred_element_type=F32)
        xf = xb.astype(F32)
        sq = xf * xf
        sq = (sq[:, 0:128] + sq[:, 128:256]) + (sq[:, 256:384] + sq[:, 384:512])
        mean = y[:, 128:256]
        var = jnp.maximum(jnp.sum(sq, axis=1, keepdims=True) * (1.0 / D) - mean * mean, 0.0)
        feats = (y[:, 0:128] - cs[...] * mean) * lax.rsqrt(var + 1e-05)
        fbuf[...] = (feats + one_at_64).astype(BF16)

    def slices(fbuf):
        feats = fbuf[...]
        logits = contract_lanes(pT[...], feats)
        w = softmax_weights(logits[0:G], logits[G : G + 1] + logits[G + 1 : G + 2])
        acc[...] += jnp.dot(w, feats, preferred_element_type=F32)

    project(0, f0)

    def two_blocks(j, _):
        @pl.when(j == 1)
        def _():
            pl.semaphore_wait(barrier, 1 + 15 + 7)
            weights_start()

        slices(f0)
        project(2 * j + 1, f1)
        slices(f1)
        project(2 * j + 2, f0)
        return 0

    lax.fori_loop(0, NBLK // 2, two_blocks, 0)
    slices(f0)

    pair[0] = acc[...]
    pair_copy = to(pair.at[0], pair_sem, (partner, z), pair.at[1])
    pair_copy.start()
    weights_onward(0)
    pair_copy.wait_recv()
    plane[0] = pair[0] + pair[1]
    for r in range(1, 16):
        to(plane.at[0], plane_sem, (pts_at(*PLANE[r]), z), plane.at[r]).start()
    plane_all = to(plane.at[pl.ds(1, 15)], plane_sem, (partner, z))

    own = pl.multiple_of(z * OWN, 128)

    def own_norm(t, _):
        rows = xv[pl.ds(pl.multiple_of(own + t * 128, 128), 128), :].astype(F32)
        centred = rows - jnp.mean(rows, axis=1, keepdims=True)
        var = jnp.mean(centred * centred, axis=1, keepdims=True)
        nown[pl.ds(pl.multiple_of(t * 128, 128), 128), :] = (centred * lax.rsqrt(var + 1e-05)).astype(BF16)
        return 0

    lax.fori_loop(0, OWN // 128, own_norm, 0)
    weights_onward(1)
    weights_far(0)
    weights_done(0)
    yall[...] = contract_lanes(wall[0].reshape(D, D), nown[...]).astype(BF16)

    plane_all.wait_recv()
    sums = jnp.sum(plane[...], axis=0)
    tokens = sums[:, 0:DH] / (sums[:, DH : DH + 1] + 1e-05)
    queries = jnp.dot(tokens, qkv_ref[0], preferred_element_type=F32, precision=HIGH)
    keys = jnp.dot(tokens, qkv_ref[1], preferred_element_type=F32, precision=HIGH)
    values = jnp.dot(
        tokens, jnp.concatenate([qkv_ref[2], jnp.zeros((DH, DH), F32)], axis=1),
        preferred_element_type=F32, precision=HIGH,
    )
    scores = contract_lanes(queries, keys, precision=HIGH) * 0.125
    e = jnp.exp(scores - jnp.max(scores, axis=1, keepdims=True))
    attend = e / jnp.sum(e, axis=1, keepdims=True)
    zbuf[z] = jnp.dot(attend, values, preferred_element_type=F32, precision=HIGH).astype(BF16)

    for dz in range(1, H):
        to(zbuf.at[z], z_sem, (pts, z_at(dz))).start()
    z_all = to(zbuf.at[pl.ds(0, H - 1)], z_sem, (partner, z))

    def own_head(h, _):
        feats = yall[pl.ds(pl.multiple_of(h * DH, DH), DH), :]
        logits = jnp.dot(pT[:, 0:DH], feats, preferred_element_type=F32)
        w = softmax_weights(logits[0:G], logits[G : G + 1] + logits[G + 1 : G + 2])
        wT[pl.ds(pl.multiple_of(h * G, G), G), :] = w
        return 0

    lax.fori_loop(0, H, own_head, 0)
    weights_far(1)
    wn[...] = wT[...].T
    weights_done(1)
    z_all.wait_recv()

    for h in range(H):
        mbuf[h * G : (h + 1) * G, :] = jnp.dot(
            zbuf[h][:, 0:DH], wall[1, h].reshape(DH, D), preferred_element_type=F32
        ).astype(BF16)

    def tail_rows(t, _):
        rows = pl.ds(pl.multiple_of(t * TBLK, 32), TBLK)
        x_rows = xv[pl.ds(pl.multiple_of(own + t * TBLK, 32), TBLK), :].astype(F32)
        midway = x_rows + jnp.dot(wn[rows, :], mbuf[...], preferred_element_type=F32)
        centred = midway - jnp.mean(midway, axis=1, keepdims=True)
        var = jnp.mean(centred * centred, axis=1, keepdims=True)
        normed = (centred * lax.rsqrt(var + 1e-05)).astype(BF16)
        hidden = jnp.dot(normed, wall[2].reshape(D, D), preferred_element_type=F32)
        hidden = jax.nn.gelu(hidden).astype(BF16)
        out = midway + jnp.dot(hidden, wall[3].reshape(D, D), preferred_element_type=F32)
        out_ref[rows, :] = out.astype(BF16)
        return 0

    lax.fori_loop(0, OWN // TBLK, tail_rows, 0)

    for g in range(2):
        of_size(g, 4, own_sem).wait_send()
        of_size(g, 3, far_sem).wait_send()
        of_size(g, 7, d2d_sem).wait_send()
    pair_copy.wait_send()
    plane_all.wait_send()
    z_all.wait_send()


OUT = pltpu.VMEM((OWN, D), BF16)


def local(x, entry, partition, sharpness, qkv, exit_matrix, widening, narrowing):
    hbm = pl.BlockSpec(memory_space=pl.ANY)
    vmem = pl.BlockSpec(memory_space=pltpu.VMEM)
    dma = pltpu.SemaphoreType.DMA
    return pl.pallas_call(
        kernel,
        out_shape=OUT,
        in_specs=[hbm, hbm, vmem, vmem, vmem, hbm, hbm, hbm],
        out_specs=vmem,
        scratch_shapes=[
            pltpu.VMEM((ROWS, D), BF16),
            pltpu.VMEM((DH, D), BF16),
            pltpu.VMEM((D, 256), BF16),
            pltpu.VMEM((G + 16, 128), BF16),
            pltpu.VMEM((1, 128), F32),
            pltpu.VMEM((BLK, 128), BF16),
            pltpu.VMEM((BLK, 128), BF16),
            pltpu.VMEM((G, 128), F32),
            pltpu.VMEM((4, H, 2, HALF, D), BF16),
            pltpu.VMEM((OWN, D), BF16),
            pltpu.VMEM((H * G, OWN), BF16),
            pltpu.VMEM((OWN, H * G), BF16),
            pltpu.VMEM((H * G, D), BF16),
            pltpu.VMEM((D, OWN), BF16),
            pltpu.VMEM((2, G, 128), F32),
            pltpu.VMEM((16, G, 128), F32),
            pltpu.VMEM((H, G, 128), BF16),
            dma((NBLK,)),
            dma((9,)),
            dma((2, 2)),
            dma((2, 2)),
            dma((2, 2)),
            dma((2,)),
            dma((2,)),
            dma((2,)),
        ],
        compiler_params=pltpu.CompilerParams(
            collective_id=0, has_side_effects=True, vmem_limit_bytes=60 * 2**20
        ),
    )(x, entry.T, partition.T, sharpness.reshape(1, DH), qkv, exit_matrix, widening, narrowing)


def solution(mesh):
    placed = (
        P("pts", None), P(None, "wid"), P(), P(), P(),
        P("wid", None), P("wid", None), P("wid", None),
    )
    return jax.shard_map(
        local, mesh=mesh, in_specs=placed, out_specs=P(("pts", "wid"), None), check_vma=False
    )
```

time: 50 us -> 41.7 us (0.83)
  local copies, waits for them, and re-layouts: 5.53 us -> 1.1 us
  Pallas kernels: 43.9 us -> 40.5 us
    unnamed x3 -> x1, local copies, waits for them, and re-layouts: 5.53 us -> 1.1 us
    pallas_call x1, Pallas kernels: 43.9 us -> 40.5 us  [local(): pl.pallas_call(kernel, out_shape=OUT, in_specs=[hbm, hbm, vmem, vmem, vme...]
where the time goes in v2:
time: 41.7 us; the launch traced here: 41.6 us
  Pallas kernels  40.5 us (97%)
  local copies, waits for them, and re-layouts  1.1 us (3%)
    pallas_call x1, Pallas kernels, local(): pl.pallas_call(kernel, out_shape=OUT, in_specs=[hbm, hbm, vmem, vmem, vme...  40.5 us
    unnamed x1, local copies, waits for them, and re-layouts  1.1 us

profile of v2, /device:TPU:1, one launch (start us, length us, event | category | flops | bytes accessed | tf_op | source)
XLA Modules:
  0.0 41.6 jit_solution(6474204841270356228)
XLA Ops:
  0.0 40.5 %shard_map.82 = bf16[1408,512]{1,0:T(8,128)(2,1)S(1)} custom-call(bf16[11264,512]{1,0:T(8,128)(2,1)} %x_hbm.1, bf16[64,512]{1,0:T(8,128)(2,1)} %bitcast.3, bf16[32,64]{1,0:T(8,128)(2,1)} %bitcast.4, f32[1,64]{1,0:T(1,128)} %bitcast.5, f32[3,64,64]{2,1,0:T(8,128)} %qkv_ref.1, bf16[64,512]{1,0:T(8,128)(2,1)} %exit_hbm.1, bf16[64,512]{1,0:T(8,128)(2,1)} %wide_hbm.1, ...), custom_call_target="tpu_custom_call" | custom-call | tf_op jit(solution)/shard_map/pallas_call | solution.py:264
  40.5 1.1 %copy.10 = bf16[1408,512]{1,0:T(8,128)(2,1)} copy(bf16[1408,512]{1,0:T(8,128)(2,1)S(1)} %shard_map.82) | data formatting | bytes 2883584

commit v3 on v2

--- a/solution.py
+++ b/solution.py
@@ -38,9 +38,9 @@
 
 
 def kernel(
-    x_hbm, entry_hbm, part_ref, sharp_ref, qkv_ref, exit_hbm, wide_hbm, narrow_hbm,
+    x_hbm, entry_hbm, part_hbm, sharp_hbm, qkv_hbm, exit_hbm, wide_hbm, narrow_hbm,
     out_ref,
-    xv, eh, waug, pT, cs, f0, f1, acc, wall, nown, wT, wn, mbuf, yall,
+    xv, eh, part_ref, sharp_ref, qkv_ref, waug, pT, cs, f0, f1, acc, wall, nown, wT, wn, mbuf, yall, m0, m1, n0, n1,
     pair, plane, zbuf,
     x_sem, in_sem, own_sem, far_sem, d2d_sem, pair_sem, plane_sem, z_sem,
 ):
@@ -61,7 +61,14 @@
         )
 
     entry_copy = pltpu.make_async_copy(entry_hbm, eh, in_sem.at[0])
+    small_copies = [
+        pltpu.make_async_copy(part_hbm, part_ref, in_sem.at[9]),
+        pltpu.make_async_copy(sharp_hbm, sharp_ref, in_sem.at[10]),
+    ]
+    qkv_copy = pltpu.make_async_copy(qkv_hbm, qkv_ref, in_sem.at[11])
     entry_copy.start()
+    for copy in small_copies:
+        copy.start()
     x_copy(0).start()
     own_copies = []
     for k, ref in enumerate((entry_hbm, exit_hbm, wide_hbm, narrow_hbm)):
@@ -79,6 +86,8 @@
     for dz in range(1, H):
         pl.semaphore_signal(barrier, inc=1, device_id=(pts, z_at(dz)), device_id_type=MESH)
 
+    for copy in small_copies:
+        copy.wait()
     sharp = jnp.broadcast_to(sharp_ref[...], (16, DH))
     sharp_hi = sharp.astype(BF16).astype(F32)
     row16 = lax.broadcasted_iota(jnp.int32, (16, DH), 0)
@@ -93,6 +102,7 @@
         x_copy(i).start()
     for copy in own_copies:
         copy.start()
+    qkv_copy.start()
     head = jnp.concatenate([eh[...].astype(F32), jnp.zeros((DH, D), F32)], axis=0).T
     cs[...] = jnp.sum(head, axis=0, keepdims=True)
     waug[:, 0:128] = head.astype(BF16)
@@ -135,7 +145,6 @@
         of_size(g, 7, d2d_sem).wait_recv()
 
     def project(i, fbuf):
-        x_copy(i).wait()
         xb = xv[pl.ds(pl.multiple_of(i * BLK, BLK), BLK), :]
         y = jnp.dot(xb, waug[...], preferred_element_type=F32)
         xf = xb.astype(F32)
@@ -152,6 +161,7 @@
         w = softmax_weights(logits[0:G], logits[G : G + 1] + logits[G + 1 : G + 2])
         acc[...] += jnp.dot(w, feats, preferred_element_type=F32)
 
+    x_copy(0).wait()
     project(0, f0)
 
     def two_blocks(j, _):
@@ -160,6 +170,8 @@
             pl.semaphore_wait(barrier, 1 + 15 + 7)
             weights_start()
 
+        x_copy(2 * j + 1).wait()
+        x_copy(2 * j + 2).wait()
         slices(f0)
         project(2 * j + 1, f1)
         slices(f1)
@@ -182,18 +194,19 @@
     own = pl.multiple_of(z * OWN, 128)
 
     def own_norm(t, _):
-        rows = xv[pl.ds(pl.multiple_of(own + t * 128, 128), 128), :].astype(F32)
+        rows = xv[pl.ds(pl.multiple_of(own + t * TBLK, 32), TBLK), :].astype(F32)
         centred = rows - jnp.mean(rows, axis=1, keepdims=True)
         var = jnp.mean(centred * centred, axis=1, keepdims=True)
-        nown[pl.ds(pl.multiple_of(t * 128, 128), 128), :] = (centred * lax.rsqrt(var + 1e-05)).astype(BF16)
+        nown[pl.ds(pl.multiple_of(t * TBLK, 32), TBLK), :] = (centred * lax.rsqrt(var + 1e-05)).astype(BF16)
         return 0
 
-    lax.fori_loop(0, OWN // 128, own_norm, 0)
+    lax.fori_loop(0, OWN // TBLK, own_norm, 0)
     weights_onward(1)
     weights_far(0)
     weights_done(0)
     yall[...] = contract_lanes(wall[0].reshape(D, D), nown[...]).astype(BF16)
 
+    qkv_copy.wait()
     plane_all.wait_recv()
     sums = jnp.sum(plane[...], axis=0)
     tokens = sums[:, 0:DH] / (sums[:, DH : DH + 1] + 1e-05)
@@ -212,15 +225,13 @@
         to(zbuf.at[z], z_sem, (pts, z_at(dz))).start()
     z_all = to(zbuf.at[pl.ds(0, H - 1)], z_sem, (partner, z))
 
-    def own_head(h, _):
-        feats = yall[pl.ds(pl.multiple_of(h * DH, DH), DH), :]
-        logits = jnp.dot(pT[:, 0:DH], feats, preferred_element_type=F32)
-        w = softmax_weights(logits[0:G], logits[G : G + 1] + logits[G + 1 : G + 2])
-        wT[pl.ds(pl.multiple_of(h * G, G), G), :] = w
-        return 0
-
-    lax.fori_loop(0, H, own_head, 0)
-    weights_far(1)
+    for h in range(H):
+        if h == H // 2:
+            weights_far(1)
+        logits = jnp.dot(pT[:, 0:DH], yall[h * DH : (h + 1) * DH, :], preferred_element_type=F32)
+        wT[h * G : (h + 1) * G, :] = softmax_weights(
+            logits[0:G], logits[G : G + 1] + logits[G + 1 : G + 2]
+        )
     wn[...] = wT[...].T
     weights_done(1)
     z_all.wait_recv()
@@ -230,20 +241,26 @@
             zbuf[h][:, 0:DH], wall[1, h].reshape(DH, D), preferred_element_type=F32
         ).astype(BF16)
 
-    def tail_rows(t, _):
-        rows = pl.ds(pl.multiple_of(t * TBLK, 32), TBLK)
+    def mix(t, mid, normed):
         x_rows = xv[pl.ds(pl.multiple_of(own + t * TBLK, 32), TBLK), :].astype(F32)
-        midway = x_rows + jnp.dot(wn[rows, :], mbuf[...], preferred_element_type=F32)
+        midway = x_rows + jnp.dot(wn[t * TBLK : (t + 1) * TBLK, :], mbuf[...], preferred_element_type=F32)
         centred = midway - jnp.mean(midway, axis=1, keepdims=True)
         var = jnp.mean(centred * centred, axis=1, keepdims=True)
-        normed = (centred * lax.rsqrt(var + 1e-05)).astype(BF16)
-        hidden = jnp.dot(normed, wall[2].reshape(D, D), preferred_element_type=F32)
+        mid[...] = midway
+        normed[...] = (centred * lax.rsqrt(var + 1e-05)).astype(BF16)
+
+    def feed(t, mid, normed):
+        hidden = jnp.dot(normed[...], wall[2].reshape(D, D), preferred_element_type=F32)
         hidden = jax.nn.gelu(hidden).astype(BF16)
-        out = midway + jnp.dot(hidden, wall[3].reshape(D, D), preferred_element_type=F32)
-        out_ref[rows, :] = out.astype(BF16)
-        return 0
-
-    lax.fori_loop(0, OWN // TBLK, tail_rows, 0)
+        out = mid[...] + jnp.dot(hidden, wall[3].reshape(D, D), preferred_element_type=F32)
+        out_ref[t * TBLK : (t + 1) * TBLK, :] = out.astype(BF16)
+
+    stage = ((m0, n0), (m1, n1))
+    mix(0, *stage[0])
+    for t in range(OWN // TBLK):
+        if t + 1 < OWN // TBLK:
+            mix(t + 1, *stage[(t + 1) % 2])
+        feed(t, *stage[t % 2])
 
     for g in range(2):
         of_size(g, 4, own_sem).wait_send()
@@ -264,11 +281,14 @@
     return pl.pallas_call(
         kernel,
         out_shape=OUT,
-        in_specs=[hbm, hbm, vmem, vmem, vmem, hbm, hbm, hbm],
+        in_specs=[hbm] * 8,
         out_specs=vmem,
         scratch_shapes=[
             pltpu.VMEM((ROWS, D), BF16),
             pltpu.VMEM((DH, D), BF16),
+            pltpu.VMEM((G, DH), BF16),
+            pltpu.VMEM((1, DH), F32),
+            pltpu.VMEM((3, DH, DH), F32),
             pltpu.VMEM((D, 256), BF16),
             pltpu.VMEM((G + 16, 128), BF16),
             pltpu.VMEM((1, 128), F32),
@@ -281,11 +301,15 @@
             pltpu.VMEM((OWN, H * G), BF16),
             pltpu.VMEM((H * G, D), BF16),
             pltpu.VMEM((D, OWN), BF16),
+            pltpu.VMEM((TBLK, D), F32),
+            pltpu.VMEM((TBLK, D), F32),
+            pltpu.VMEM((TBLK, D), BF16),
+            pltpu.VMEM((TBLK, D), BF16),
             pltpu.VMEM((2, G, 128), F32),
             pltpu.VMEM((16, G, 128), F32),
             pltpu.VMEM((H, G, 128), BF16),
             dma((NBLK,)),
-            dma((9,)),
+            dma((12,)),
             dma((2, 2)),
             dma((2, 2)),
             dma((2, 2)),

time: 41.7 us -> 38 us (0.911)
  Pallas kernels: 40.5 us -> 36.8 us
    pallas_call x1, Pallas kernels: 40.5 us -> 36.8 us  [local(): pl.pallas_call(kernel, out_shape=OUT, in_specs=[hbm] * 8, out_specs=vmem,...]
where the time goes in v3:
time: 38 us; the launch traced here: 37.9 us
  Pallas kernels  36.8 us (97%)
  local copies, waits for them, and re-layouts  1.1 us (3%)
    pallas_call x1, Pallas kernels, local(): pl.pallas_call(kernel, out_shape=OUT, in_specs=[hbm] * 8, out_specs=vmem,...  36.8 us
    unnamed x1, local copies, waits for them, and re-layouts  1.1 us

profile of v3, /device:TPU:1, one launch (start us, length us, event | category | flops | bytes accessed | tf_op | source)
XLA Modules:
  0.0 37.9 jit_solution(6791672408055987210)
XLA Ops:
  0.0 36.8 %shard_map.82 = bf16[1408,512]{1,0:T(8,128)(2,1)S(1)} custom-call(bf16[11264,512]{1,0:T(8,128)(2,1)} %x_hbm.1, bf16[64,512]{1,0:T(8,128)(2,1)} %bitcast.3, bf16[32,64]{1,0:T(8,128)(2,1)} %bitcast.4, f32[1,64]{1,0:T(1,128)} %bitcast.5, f32[3,64,64]{2,1,0:T(8,128)} %qkv_hbm.1, bf16[64,512]{1,0:T(8,128)(2,1)} %exit_hbm.1, bf16[64,512]{1,0:T(8,128)(2,1)} %wide_hbm.1, ...), custom_call_target="tpu_custom_call" | custom-call | tf_op jit(solution)/shard_map/pallas_call | solution.py:281
  36.8 1.1 %copy.10 = bf16[1408,512]{1,0:T(8,128)(2,1)} copy(bf16[1408,512]{1,0:T(8,128)(2,1)S(1)} %shard_map.82) | data formatting | bytes 2883584

commit v4 on v3

--- a/solution.py
+++ b/solution.py
@@ -14,7 +14,8 @@
 D, H, DH, G = 512, 8, 64, 32
 ROWS = 11264
 OWN = 1408
-BLK = 1024
+BLK = 1408
+SUB = 352
 NBLK = ROWS // BLK
 TBLK = 352
 HALF = DH // 2
@@ -30,9 +31,12 @@
     )
 
 
-def softmax_weights(logits, temperature_logit):
-    soft = jnp.maximum(temperature_logit, 0.0) + jnp.log(1.0 + jnp.exp(-jnp.abs(temperature_logit)))
-    scaled = logits * (1.0 / (0.5 + soft))
+def inverse_temperature(logit):
+    return 1.0 / (0.5 + jnp.maximum(logit, 0.0) + jnp.log(1.0 + jnp.exp(-jnp.abs(logit))))
+
+
+def softmax_weights(logits):
+    scaled = logits[0:G] * inverse_temperature(logits[G : G + 1] + logits[G + 1 : G + 2])
     e = jnp.exp(scaled - jnp.max(scaled, axis=0, keepdims=True))
     return (e * (1.0 / jnp.sum(e, axis=0, keepdims=True))).astype(BF16)
 
@@ -144,8 +148,11 @@
     def weights_done(g):
         of_size(g, 7, d2d_sem).wait_recv()
 
-    def project(i, fbuf):
-        xb = xv[pl.ds(pl.multiple_of(i * BLK, BLK), BLK), :]
+    def project(i, q, fbuf):
+        start = i * BLK + q * SUB
+        if not isinstance(start, int):
+            start = pl.multiple_of(start, SUB)
+        xb = xv[pl.ds(start, SUB), :]
         y = jnp.dot(xb, waug[...], preferred_element_type=F32)
         xf = xb.astype(F32)
         sq = xf * xf
@@ -153,16 +160,28 @@
         mean = y[:, 128:256]
         var = jnp.maximum(jnp.sum(sq, axis=1, keepdims=True) * (1.0 / D) - mean * mean, 0.0)
         feats = (y[:, 0:128] - cs[...] * mean) * lax.rsqrt(var + 1e-05)
-        fbuf[...] = (feats + one_at_64).astype(BF16)
+        fbuf[q * SUB : (q + 1) * SUB, :] = (feats + one_at_64).astype(BF16)
 
     def slices(fbuf):
-        feats = fbuf[...]
-        logits = contract_lanes(pT[...], feats)
-        w = softmax_weights(logits[0:G], logits[G : G + 1] + logits[G + 1 : G + 2])
-        acc[...] += jnp.dot(w, feats, preferred_element_type=F32)
+        logits = contract_lanes(pT[...], fbuf[...])
+        yield
+        scaled = logits[0:G] * inverse_temperature(logits[G : G + 1] + logits[G + 1 : G + 2])
+        e = jnp.exp(scaled - jnp.max(scaled, axis=0, keepdims=True))
+        yield
+        w = (e * (1.0 / jnp.sum(e, axis=0, keepdims=True))).astype(BF16)
+        yield
+        acc[...] += jnp.dot(w, fbuf[...], preferred_element_type=F32)
+        yield
+
+    def project_and_slices(i, fbuf, other):
+        steps = slices(other)
+        for q in range(BLK // SUB):
+            project(i, q, fbuf)
+            next(steps)
 
     x_copy(0).wait()
-    project(0, f0)
+    for q in range(BLK // SUB):
+        project(0, q, f0)
 
     def two_blocks(j, _):
         @pl.when(j == 1)
@@ -172,14 +191,15 @@
 
         x_copy(2 * j + 1).wait()
         x_copy(2 * j + 2).wait()
-        slices(f0)
-        project(2 * j + 1, f1)
-        slices(f1)
-        project(2 * j + 2, f0)
+        project_and_slices(2 * j + 1, f1, f0)
+        project_and_slices(2 * j + 2, f0, f1)
         return 0
 
-    lax.fori_loop(0, NBLK // 2, two_blocks, 0)
-    slices(f0)
+    lax.fori_loop(0, NBLK // 2 - 1, two_blocks, 0)
+    x_copy(NBLK - 1).wait()
+    project_and_slices(NBLK - 1, f1, f0)
+    for _ in slices(f1):
+        pass
 
     pair[0] = acc[...]
     pair_copy = to(pair.at[0], pair_sem, (partner, z), pair.at[1])
@@ -203,8 +223,6 @@
     lax.fori_loop(0, OWN // TBLK, own_norm, 0)
     weights_onward(1)
     weights_far(0)
-    weights_done(0)
-    yall[...] = contract_lanes(wall[0].reshape(D, D), nown[...]).astype(BF16)
 
     qkv_copy.wait()
     plane_all.wait_recv()
@@ -225,13 +243,13 @@
         to(zbuf.at[z], z_sem, (pts, z_at(dz))).start()
     z_all = to(zbuf.at[pl.ds(0, H - 1)], z_sem, (partner, z))
 
+    weights_done(0)
+    yall[...] = contract_lanes(wall[0].reshape(D, D), nown[...]).astype(BF16)
     for h in range(H):
         if h == H // 2:
             weights_far(1)
         logits = jnp.dot(pT[:, 0:DH], yall[h * DH : (h + 1) * DH, :], preferred_element_type=F32)
-        wT[h * G : (h + 1) * G, :] = softmax_weights(
-            logits[0:G], logits[G : G + 1] + logits[G + 1 : G + 2]
-        )
+        wT[h * G : (h + 1) * G, :] = softmax_weights(logits)
     wn[...] = wT[...].T
     weights_done(1)
     z_all.wait_recv()

time: 38 us -> 34.1 us (0.90)
  Pallas kernels: 36.8 us -> 32.9 us
    pallas_call x1, Pallas kernels: 36.8 us -> 32.9 us  [local(): pl.pallas_call(kernel, out_shape=OUT, in_specs=[hbm] * 8, out_specs=vmem,...]
where the time goes in v4:
time: 34.1 us; the launch traced here: 34 us
  Pallas kernels  32.9 us (96%)
  local copies, waits for them, and re-layouts  1.1 us (3%)
    pallas_call x1, Pallas kernels, local(): pl.pallas_call(kernel, out_shape=OUT, in_specs=[hbm] * 8, out_specs=vmem,...  32.9 us
    unnamed x1, local copies, waits for them, and re-layouts  1.1 us

profile of v4, /device:TPU:1, one launch (start us, length us, event | category | flops | bytes accessed | tf_op | source)
XLA Modules:
  0.0 34.0 jit_solution(11504880356116669801)
XLA Ops:
  0.0 32.9 %shard_map.82 = bf16[1408,512]{1,0:T(8,128)(2,1)S(1)} custom-call(bf16[11264,512]{1,0:T(8,128)(2,1)} %x_hbm.1, bf16[64,512]{1,0:T(8,128)(2,1)} %bitcast.3, bf16[32,64]{1,0:T(8,128)(2,1)} %bitcast.4, f32[1,64]{1,0:T(1,128)} %bitcast.5, f32[3,64,64]{2,1,0:T(8,128)} %qkv_hbm.1, bf16[64,512]{1,0:T(8,128)(2,1)} %exit_hbm.1, bf16[64,512]{1,0:T(8,128)(2,1)} %wide_hbm.1, ...), custom_call_target="tpu_custom_call" | custom-call | tf_op jit(solution)/shard_map/pallas_call | solution.py:299
  32.9 1.1 %copy.10 = bf16[1408,512]{1,0:T(8,128)(2,1)} copy(bf16[1408,512]{1,0:T(8,128)(2,1)S(1)} %shard_map.82) | data formatting | bytes 2883584

commit v5 on v4

--- a/solution.py
+++ b/solution.py
@@ -15,14 +15,15 @@
 ROWS = 11264
 OWN = 1408
 BLK = 1408
-SUB = 352
+PAIRS = BLK // 2
+DOT = 352
+SUB = 176
 NBLK = ROWS // BLK
-TBLK = 352
+NORM_ROWS = 352
+TBLK = 704
 HALF = DH // 2
 
 PLANE = [(dx, dy) for dx in range(4) for dy in range(4)]
-Z_NEAR = (1, -1, 2, -2)
-Z_FAR = ((-2, 1, (0, HALF)), (2, -1, (0, HALF)), (-2, 2, (0, HALF // 2)), (2, -2, (HALF // 2, HALF // 2)))
 
 
 def contract_lanes(a, b, precision=None):
@@ -46,7 +47,7 @@
     out_ref,
     xv, eh, part_ref, sharp_ref, qkv_ref, waug, pT, cs, f0, f1, acc, wall, nown, wT, wn, mbuf, yall, m0, m1, n0, n1,
     pair, plane, zbuf,
-    x_sem, in_sem, own_sem, far_sem, d2d_sem, pair_sem, plane_sem, z_sem,
+    x_sem, in_sem, own_sem, hop_sem, far_sem, d2d_sem, pair_sem, plane_sem, z_sem,
 ):
     pts, z = lax.axis_index("pts"), lax.axis_index("wid")
     core = lax.rem(pts, 2)
@@ -83,6 +84,10 @@
                 )
             )
 
+    for copy in own_copies:
+        copy.start()
+    qkv_copy.start()
+
     barrier = pltpu.get_barrier_semaphore()
     pl.semaphore_signal(barrier, inc=1, device_id=(partner, z), device_id_type=MESH)
     for dx, dy in PLANE[1:]:
@@ -97,22 +102,21 @@
     row16 = lax.broadcasted_iota(jnp.int32, (16, DH), 0)
     tail = jnp.where(row16 == 0, sharp_hi, jnp.where(row16 == 1, sharp - sharp_hi, 0.0))
     table = jnp.concatenate([part_ref[...].astype(F32), tail], axis=0)
-    pT[...] = jnp.concatenate([table, jnp.zeros((G + 16, DH), F32)], axis=1).astype(BF16)
+    blank = jnp.zeros((G + 16, DH), F32)
+    pT[0 : G + 16, :] = jnp.concatenate([table, blank], axis=1).astype(BF16)
+    pT[G + 16 :, :] = jnp.concatenate([blank, table], axis=1).astype(BF16)
     acc[...] = jnp.zeros_like(acc)
-    one_at_64 = (lax.broadcasted_iota(jnp.int32, (1, 128), 1) == DH).astype(F32)
-
-    entry_copy.wait()
+
     for i in range(1, NBLK):
         x_copy(i).start()
-    for copy in own_copies:
-        copy.start()
-    qkv_copy.start()
-    head = jnp.concatenate([eh[...].astype(F32), jnp.zeros((DH, D), F32)], axis=0).T
-    cs[...] = jnp.sum(head, axis=0, keepdims=True)
-    waug[:, 0:128] = head.astype(BF16)
-    waug[:, 128:256] = jnp.full((D, 128), 1.0 / D, BF16)
-
-    mats = (pl.ds(0, 1), pl.ds(1, 3))
+    entry_copy.wait()
+    head = eh[...].astype(F32)
+    low = lax.broadcasted_iota(jnp.int32, (D, 128), 1) < DH
+    both = jnp.concatenate([head, head], axis=0).T
+    cs[...] = jnp.sum(both, axis=0, keepdims=True)
+    for half, lanes in ((0, low), (1, jnp.logical_not(low))):
+        waug[half * D : (half + 1) * D, 0:128] = jnp.where(lanes, both, 0.0).astype(BF16)
+        waug[half * D : (half + 1) * D, 128:256] = jnp.where(lanes, 1.0 / D, 0.0).astype(BF16)
 
     def to(ref, sems, device, target=None):
         return pltpu.make_async_remote_copy(
@@ -121,73 +125,100 @@
         )
 
     def half_of(g, offset, half, rows=pl.ds(0, HALF)):
-        return wall.at[mats[g], z_at(offset), half, rows]
+        return wall.at[g, z_at(offset), half, rows]
 
     def of_size(g, n, sems):
-        return to(wall.at[mats[g], pl.ds(0, n), 0], sems.at[g], (partner, z))
-
-    def weights_start():
+        return to(wall.at[g, pl.ds(0, n), 0], sems.at[g], (partner, z))
+
+    def to_partner(g, offsets):
+        for offset in offsets:
+            to(half_of(g, offset, core), d2d_sem.at[g], (partner, z)).start()
+
+    def weights_1():
         for copy in own_copies:
             copy.wait()
-        for g in range(2):
-            for dz in Z_NEAR:
-                to(half_of(g, 0, core), own_sem.at[g], (pts, z_at(dz))).start()
-
-    def weights_onward(g):
-        of_size(g, 4, own_sem).wait_recv()
-        for source, dz, rows in Z_FAR:
-            to(half_of(g, source, core, pl.ds(*rows)), far_sem.at[g], (pts, z_at(dz))).start()
-        for offset in Z_NEAR:
-            to(half_of(g, offset, core), d2d_sem.at[g], (partner, z)).start()
+        for g in range(4):
+            for d in (1, -1):
+                to(half_of(g, 0, core), own_sem.at[g], (pts, z_at(d))).start()
+
+    def weights_2(g):
+        of_size(g, 2, own_sem).wait_recv()
+        for d in (1, -1):
+            to(half_of(g, -d, core), hop_sem.at[g], (pts, z_at(d))).start()
+
+    def weights_3(g):
+        of_size(g, 2, hop_sem).wait_recv()
+        for d, first in ((1, 0), (-1, HALF // 2)):
+            to(half_of(g, -2 * d, core), far_sem.at[g], (pts, z_at(d))).start()
+            rows = pl.ds(first, HALF // 2)
+            to(half_of(g, -2 * d, core, rows), far_sem.at[g], (pts, z_at(2 * d))).start()
+        to_partner(g, (1, -1, 2, -2))
 
     def weights_far(g):
         of_size(g, 3, far_sem).wait_recv()
-        for offset in (3, -3, 4):
-            to(half_of(g, offset, core), d2d_sem.at[g], (partner, z)).start()
+        to_partner(g, (3, -3, 4))
 
     def weights_done(g):
         of_size(g, 7, d2d_sem).wait_recv()
 
     def project(i, q, fbuf):
-        start = i * BLK + q * SUB
+        start = i * BLK + q * DOT
         if not isinstance(start, int):
-            start = pl.multiple_of(start, SUB)
-        xb = xv[pl.ds(start, SUB), :]
-        y = jnp.dot(xb, waug[...], preferred_element_type=F32)
-        xf = xb.astype(F32)
-        sq = xf * xf
-        sq = (sq[:, 0:128] + sq[:, 128:256]) + (sq[:, 256:384] + sq[:, 384:512])
-        mean = y[:, 128:256]
-        var = jnp.maximum(jnp.sum(sq, axis=1, keepdims=True) * (1.0 / D) - mean * mean, 0.0)
-        feats = (y[:, 0:128] - cs[...] * mean) * lax.rsqrt(var + 1e-05)
-        fbuf[q * SUB : (q + 1) * SUB, :] = (feats + one_at_64).astype(BF16)
+            start = pl.multiple_of(start, 32)
+        first = xv[pl.ds(start, DOT), :]
+        second = xv[pl.ds(start + PAIRS, DOT), :]
+        y = jnp.dot(jnp.concatenate([first, second], axis=1), waug[...], preferred_element_type=F32)
+        lower = lax.broadcasted_iota(jnp.int32, (SUB, 128), 1) < DH
+
+        def square_sums(rows):
+            sq = rows.astype(F32)
+            sq = sq * sq
+            sq = (sq[:, 0:128] + sq[:, 128:256]) + (sq[:, 256:384] + sq[:, 384:512])
+            return jnp.sum(sq, axis=1, keepdims=True)
+
+        for r in range(0, DOT, SUB):
+            rows = slice(r, r + SUB)
+            squares = jnp.where(lower, square_sums(first[rows]), square_sums(second[rows]))
+            mean = y[rows, 128:256]
+            var = jnp.maximum(squares * (1.0 / D) - mean * mean, 0.0)
+            feats = (y[rows, 0:128] - cs[...] * mean) * lax.rsqrt(var + 1e-05)
+            fbuf[q * DOT + r : q * DOT + r + SUB, :] = feats.astype(BF16)
+            yield
 
     def slices(fbuf):
         logits = contract_lanes(pT[...], fbuf[...])
         yield
-        scaled = logits[0:G] * inverse_temperature(logits[G : G + 1] + logits[G + 1 : G + 2])
-        e = jnp.exp(scaled - jnp.max(scaled, axis=0, keepdims=True))
+        exps = []
+        for top in (0, G + 16):
+            scaled = logits[top : top + G] * inverse_temperature(
+                logits[top + G : top + G + 1] + logits[top + G + 1 : top + G + 2]
+            )
+            exps.append(jnp.exp(scaled - jnp.max(scaled, axis=0, keepdims=True)))
         yield
-        w = (e * (1.0 / jnp.sum(e, axis=0, keepdims=True))).astype(BF16)
+        w = [(e * (1.0 / jnp.sum(e, axis=0, keepdims=True))).astype(BF16) for e in exps]
         yield
-        acc[...] += jnp.dot(w, fbuf[...], preferred_element_type=F32)
+        with_ones = jnp.concatenate([fbuf[...], jnp.ones((PAIRS, 128), BF16)], axis=1)
+        acc[...] += jnp.dot(jnp.concatenate(w, axis=0), with_ones, preferred_element_type=F32)
         yield
 
     def project_and_slices(i, fbuf, other):
         steps = slices(other)
-        for q in range(BLK // SUB):
-            project(i, q, fbuf)
-            next(steps)
+        for q in range(PAIRS // DOT):
+            for _ in project(i, q, fbuf):
+                next(steps)
 
     x_copy(0).wait()
-    for q in range(BLK // SUB):
-        project(0, q, f0)
+    for q in range(PAIRS // DOT):
+        for _ in project(0, q, f0):
+            pass
+
+    start_at = (z < 1).astype(jnp.int32) + (z < 4).astype(jnp.int32)
 
     def two_blocks(j, _):
-        @pl.when(j == 1)
+        @pl.when(j == start_at)
         def _():
             pl.semaphore_wait(barrier, 1 + 15 + 7)
-            weights_start()
+            weights_1()
 
         x_copy(2 * j + 1).wait()
         x_copy(2 * j + 2).wait()
@@ -196,32 +227,39 @@
         return 0
 
     lax.fori_loop(0, NBLK // 2 - 1, two_blocks, 0)
+    weights_2(0)
+    weights_2(1)
     x_copy(NBLK - 1).wait()
     project_and_slices(NBLK - 1, f1, f0)
+    weights_2(2)
+    weights_2(3)
     for _ in slices(f1):
         pass
 
-    pair[0] = acc[...]
+    lane = lax.broadcasted_iota(jnp.int32, (G, 128), 1)
+    numerator = acc[0:G, 0:128] + pltpu.roll(acc[G:, 0:128], DH, axis=1)
+    pair[0] = jnp.where(lane < DH, numerator, acc[0:G, 128:256] + acc[G:, 128:256])
     pair_copy = to(pair.at[0], pair_sem, (partner, z), pair.at[1])
     pair_copy.start()
-    weights_onward(0)
     pair_copy.wait_recv()
     plane[0] = pair[0] + pair[1]
     for r in range(1, 16):
         to(plane.at[0], plane_sem, (pts_at(*PLANE[r]), z), plane.at[r]).start()
     plane_all = to(plane.at[pl.ds(1, 15)], plane_sem, (partner, z))
 
+    weights_3(0)
     own = pl.multiple_of(z * OWN, 128)
 
     def own_norm(t, _):
-        rows = xv[pl.ds(pl.multiple_of(own + t * TBLK, 32), TBLK), :].astype(F32)
+        rows = xv[pl.ds(pl.multiple_of(own + t * NORM_ROWS, 32), NORM_ROWS), :].astype(F32)
         centred = rows - jnp.mean(rows, axis=1, keepdims=True)
         var = jnp.mean(centred * centred, axis=1, keepdims=True)
-        nown[pl.ds(pl.multiple_of(t * TBLK, 32), TBLK), :] = (centred * lax.rsqrt(var + 1e-05)).astype(BF16)
+        nown[pl.ds(pl.multiple_of(t * NORM_ROWS, 32), NORM_ROWS), :] = (centred * lax.rsqrt(var + 1e-05)).astype(BF16)
         return 0
 
-    lax.fori_loop(0, OWN // TBLK, own_norm, 0)
-    weights_onward(1)
+    lax.fori_loop(0, OWN // NORM_ROWS, own_norm, 0)
+    for g in range(1, 4):
+        weights_3(g)
     weights_far(0)
 
     qkv_copy.wait()
@@ -243,16 +281,19 @@
         to(zbuf.at[z], z_sem, (pts, z_at(dz))).start()
     z_all = to(zbuf.at[pl.ds(0, H - 1)], z_sem, (partner, z))
 
+    weights_far(1)
     weights_done(0)
     yall[...] = contract_lanes(wall[0].reshape(D, D), nown[...]).astype(BF16)
     for h in range(H):
-        if h == H // 2:
-            weights_far(1)
-        logits = jnp.dot(pT[:, 0:DH], yall[h * DH : (h + 1) * DH, :], preferred_element_type=F32)
+        if h == 2:
+            weights_far(2)
+        if h == 5:
+            weights_far(3)
+        logits = jnp.dot(pT[0 : G + 16, 0:DH], yall[h * DH : (h + 1) * DH, :], preferred_element_type=F32)
         wT[h * G : (h + 1) * G, :] = softmax_weights(logits)
     wn[...] = wT[...].T
+    z_all.wait_recv()
     weights_done(1)
-    z_all.wait_recv()
 
     for h in range(H):
         mbuf[h * G : (h + 1) * G, :] = jnp.dot(
@@ -275,13 +316,16 @@
 
     stage = ((m0, n0), (m1, n1))
     mix(0, *stage[0])
+    weights_done(2)
+    weights_done(3)
     for t in range(OWN // TBLK):
         if t + 1 < OWN // TBLK:
             mix(t + 1, *stage[(t + 1) % 2])
         feed(t, *stage[t % 2])
 
-    for g in range(2):
-        of_size(g, 4, own_sem).wait_send()
+    for g in range(4):
+        of_size(g, 2, own_sem).wait_send()
+        of_size(g, 2, hop_sem).wait_send()
         of_size(g, 3, far_sem).wait_send()
         of_size(g, 7, d2d_sem).wait_send()
     pair_copy.wait_send()
@@ -307,12 +351,12 @@
             pltpu.VMEM((G, DH), BF16),
             pltpu.VMEM((1, DH), F32),
             pltpu.VMEM((3, DH, DH), F32),
-            pltpu.VMEM((D, 256), BF16),
-            pltpu.VMEM((G + 16, 128), BF16),
+            pltpu.VMEM((2 * D, 256), BF16),
+            pltpu.VMEM((2 * (G + 16), 128), BF16),
             pltpu.VMEM((1, 128), F32),
-            pltpu.VMEM((BLK, 128), BF16),
-            pltpu.VMEM((BLK, 128), BF16),
-            pltpu.VMEM((G, 128), F32),
+            pltpu.VMEM((PAIRS, 128), BF16),
+            pltpu.VMEM((PAIRS, 128), BF16),
+            pltpu.VMEM((2 * G, 256), F32),
             pltpu.VMEM((4, H, 2, HALF, D), BF16),
             pltpu.VMEM((OWN, D), BF16),
             pltpu.VMEM((H * G, OWN), BF16),
@@ -328,9 +372,10 @@
             pltpu.VMEM((H, G, 128), BF16),
             dma((NBLK,)),
             dma((12,)),
-            dma((2, 2)),
-            dma((2, 2)),
-            dma((2, 2)),
+            dma((4, 2)),
+            dma((4, 2)),
+            dma((4, 2)),
+            dma((4, 2)),
             dma((2,)),
             dma((2,)),
             dma((2,)),

time: 34.1 us -> 33.7 us (0.988)
  Pallas kernels: 32.9 us -> 32.5 us
    pallas_call x1, Pallas kernels: 32.9 us -> 32.5 us  [local(): pl.pallas_call(kernel, out_shape=OUT, in_specs=[hbm] * 8, out_specs=vmem,...]
where the time goes in v5:
time: 33.7 us
  Pallas kernels  32.5 us (96%)
  local copies, waits for them, and re-layouts  1.1 us (3%)
    pallas_call x1, Pallas kernels, local(): pl.pallas_call(kernel, out_shape=OUT, in_specs=[hbm] * 8, out_specs=vmem,...  32.5 us
    unnamed x1, local copies, waits for them, and re-layouts  1.1 us

profile of v5, /device:TPU:1, one launch (start us, length us, event | category | flops | bytes accessed | tf_op | source)
XLA Modules:
  0.0 33.7 jit_solution(1599328900944175398)
XLA Ops:
  0.0 32.5 %shard_map.82 = bf16[1408,512]{1,0:T(8,128)(2,1)S(1)} custom-call(bf16[11264,512]{1,0:T(8,128)(2,1)} %x_hbm.1, bf16[64,512]{1,0:T(8,128)(2,1)} %bitcast.3, bf16[32,64]{1,0:T(8,128)(2,1)} %bitcast.4, f32[1,64]{1,0:T(1,128)} %bitcast.5, f32[3,64,64]{2,1,0:T(8,128)} %qkv_hbm.1, bf16[64,512]{1,0:T(8,128)(2,1)} %exit_hbm.1, bf16[64,512]{1,0:T(8,128)(2,1)} %wide_hbm.1, ...), custom_call_target="tpu_custom_call" | custom-call | tf_op jit(solution)/shard_map/pallas_call | solution.py:343
  32.6 1.1 %copy.10 = bf16[1408,512]{1,0:T(8,128)(2,1)} copy(bf16[1408,512]{1,0:T(8,128)(2,1)S(1)} %shard_map.82) | data formatting | bytes 2883584

commit v6 on v5

--- a/solution.py
+++ b/solution.py
@@ -168,17 +168,23 @@
         first = xv[pl.ds(start, DOT), :]
         second = xv[pl.ds(start + PAIRS, DOT), :]
         y = jnp.dot(jnp.concatenate([first, second], axis=1), waug[...], preferred_element_type=F32)
-        lower = lax.broadcasted_iota(jnp.int32, (SUB, 128), 1) < DH
-
-        def square_sums(rows):
-            sq = rows.astype(F32)
-            sq = sq * sq
-            sq = (sq[:, 0:128] + sq[:, 128:256]) + (sq[:, 256:384] + sq[:, 384:512])
-            return jnp.sum(sq, axis=1, keepdims=True)
+        lower = lax.broadcasted_iota(jnp.int32, (16, 128), 1) < DH
+
+        def square_sums(row):
+            total = None
+            for c in range(0, D, 128):
+                tile = xv[pl.ds(row, 16), c : c + 128].astype(F32)
+                total = tile * tile if total is None else total + tile * tile
+            return jnp.broadcast_to(jnp.sum(total, axis=1, keepdims=True), (16, 128))
 
         for r in range(0, DOT, SUB):
             rows = slice(r, r + SUB)
-            squares = jnp.where(lower, square_sums(first[rows]), square_sums(second[rows]))
+            squares = []
+            for k in range(r, r + SUB, 16):
+                row = start + k if isinstance(start, int) else pl.multiple_of(start + k, 16)
+                other = row + PAIRS if isinstance(start, int) else pl.multiple_of(row + PAIRS, 16)
+                squares.append(jnp.where(lower, square_sums(row), square_sums(other)))
+            squares = jnp.concatenate(squares, axis=0)
             mean = y[rows, 128:256]
             var = jnp.maximum(squares * (1.0 / D) - mean * mean, 0.0)
             feats = (y[rows, 0:128] - cs[...] * mean) * lax.rsqrt(var + 1e-05)
@@ -236,9 +242,14 @@
     for _ in slices(f1):
         pass
 
+    half_g = G // 2
     lane = lax.broadcasted_iota(jnp.int32, (G, 128), 1)
-    numerator = acc[0:G, 0:128] + pltpu.roll(acc[G:, 0:128], DH, axis=1)
-    pair[0] = jnp.where(lane < DH, numerator, acc[0:G, 128:256] + acc[G:, 128:256])
+    diagonal = lane == lax.broadcasted_iota(jnp.int32, (G, 128), 0)
+    even, odd = acc[0:G, 0:128], acc[G:, 0:128]
+    straight, crossed = even + pltpu.roll(odd, DH, axis=1), pltpu.roll(even, DH, axis=1) + odd
+    mass = acc[0:G, 128:256] + acc[G:, 128:256]
+    pair[0, 0:half_g, :] = jnp.where(lane[0:half_g] < DH, straight[0:half_g], crossed[half_g:])
+    pair[0, half_g : half_g + 1, :] = jnp.sum(jnp.where(diagonal, mass, 0.0), axis=0, keepdims=True)
     pair_copy = to(pair.at[0], pair_sem, (partner, z), pair.at[1])
     pair_copy.start()
     pair_copy.wait_recv()
@@ -265,14 +276,14 @@
     qkv_copy.wait()
     plane_all.wait_recv()
     sums = jnp.sum(plane[...], axis=0)
-    tokens = sums[:, 0:DH] / (sums[:, DH : DH + 1] + 1e-05)
-    queries = jnp.dot(tokens, qkv_ref[0], preferred_element_type=F32, precision=HIGH)
-    keys = jnp.dot(tokens, qkv_ref[1], preferred_element_type=F32, precision=HIGH)
-    values = jnp.dot(
-        tokens, jnp.concatenate([qkv_ref[2], jnp.zeros((DH, DH), F32)], axis=1),
-        preferred_element_type=F32, precision=HIGH,
-    )
-    scores = contract_lanes(queries, keys, precision=HIGH) * 0.125
+    packed = sums[0:half_g]
+    numerator = jnp.concatenate([packed, pltpu.roll(packed, DH, axis=1)], axis=0)[:, 0:DH]
+    mass = jnp.sum(jnp.where(diagonal, sums[half_g : half_g + 1], 0.0), axis=1, keepdims=True)
+    tokens = numerator / (mass + 1e-05)
+    maps = jnp.concatenate([qkv_ref[0], qkv_ref[1], qkv_ref[2], qkv_ref[2]], axis=1)
+    mapped = jnp.dot(tokens, maps, preferred_element_type=F32, precision=HIGH)
+    scores = contract_lanes(mapped[:, 0:DH], mapped[:, DH : 2 * DH], precision=HIGH) * 0.125
+    values = jnp.where((lane < DH) == (lax.rem(z, 2) == 0), mapped[:, 2 * DH : 4 * DH], 0.0)
     e = jnp.exp(scores - jnp.max(scores, axis=1, keepdims=True))
     attend = e / jnp.sum(e, axis=1, keepdims=True)
     zbuf[z] = jnp.dot(attend, values, preferred_element_type=F32, precision=HIGH).astype(BF16)
@@ -295,9 +306,14 @@
     z_all.wait_recv()
     weights_done(1)
 
-    for h in range(H):
-        mbuf[h * G : (h + 1) * G, :] = jnp.dot(
-            zbuf[h][:, 0:DH], wall[1, h].reshape(DH, D), preferred_element_type=F32
+    gap = jnp.zeros((2 * G, 128), BF16)
+    for h in range(0, H, 4):
+        first, second = (zbuf[k : k + 2].reshape(2 * G, 128) for k in (h, h + 2))
+        tokens_of_four = jnp.concatenate(
+            [jnp.concatenate([first, gap], axis=1), jnp.concatenate([gap, second], axis=1)], axis=0
+        )
+        mbuf[h * G : (h + 4) * G, :] = jnp.dot(
+            tokens_of_four, wall[1, h : h + 4].reshape(4 * DH, D), preferred_element_type=F32
         ).astype(BF16)
 
     def mix(t, mid, normed):
@@ -367,8 +383,8 @@
             pltpu.VMEM((TBLK, D), F32),
             pltpu.VMEM((TBLK, D), BF16),
             pltpu.VMEM((TBLK, D), BF16),
-            pltpu.VMEM((2, G, 128), F32),
-            pltpu.VMEM((16, G, 128), F32),
+            pltpu.VMEM((2, G // 2 + 1, 128), F32),
+            pltpu.VMEM((16, G // 2 + 1, 128), F32),
             pltpu.VMEM((H, G, 128), BF16),
             dma((NBLK,)),
             dma((12,)),

time: 33.7 us -> 33.1 us (0.982)
  Pallas kernels: 32.5 us -> 31.9 us
    pallas_call x1, Pallas kernels: 32.5 us -> 31.9 us  [local(): pl.pallas_call(kernel, out_shape=OUT, in_specs=[hbm] * 8, out_specs=vmem,...]
where the time goes in v6:
time: 33.1 us; the launch traced here: 33 us
  Pallas kernels  31.9 us (96%)
  local copies, waits for them, and re-layouts  1.1 us (3%)
    pallas_call x1, Pallas kernels, local(): pl.pallas_call(kernel, out_shape=OUT, in_specs=[hbm] * 8, out_specs=vmem,...  31.9 us
    unnamed x1, local copies, waits for them, and re-layouts  1.1 us

profile of v6, /device:TPU:1, one launch (start us, length us, event | category | flops | bytes accessed | tf_op | source)
XLA Modules:
  0.0 33.0 jit_solution(17085275160388877278)
XLA Ops:
  0.0 31.9 %shard_map.82 = bf16[1408,512]{1,0:T(8,128)(2,1)S(1)} custom-call(bf16[11264,512]{1,0:T(8,128)(2,1)} %x_hbm.1, bf16[64,512]{1,0:T(8,128)(2,1)} %bitcast.3, bf16[32,64]{1,0:T(8,128)(2,1)} %bitcast.4, f32[1,64]{1,0:T(1,128)} %bitcast.5, f32[3,64,64]{2,1,0:T(8,128)} %qkv_hbm.1, bf16[64,512]{1,0:T(8,128)(2,1)} %exit_hbm.1, bf16[64,512]{1,0:T(8,128)(2,1)} %wide_hbm.1, ...), custom_call_target="tpu_custom_call" | custom-call | tf_op jit(solution)/shard_map/pallas_call | solution.py:359
  31.9 1.1 %copy.10 = bf16[1408,512]{1,0:T(8,128)(2,1)} copy(bf16[1408,512]{1,0:T(8,128)(2,1)S(1)} %shard_map.82) | data formatting | bytes 2883584

commit v7 on v6

--- a/solution.py
+++ b/solution.py
@@ -251,12 +251,18 @@
     pair[0, 0:half_g, :] = jnp.where(lane[0:half_g] < DH, straight[0:half_g], crossed[half_g:])
     pair[0, half_g : half_g + 1, :] = jnp.sum(jnp.where(diagonal, mass, 0.0), axis=0, keepdims=True)
     pair_copy = to(pair.at[0], pair_sem, (partner, z), pair.at[1])
-    pair_copy.start()
-    pair_copy.wait_recv()
-    plane[0] = pair[0] + pair[1]
-    for r in range(1, 16):
-        to(plane.at[0], plane_sem, (pts_at(*PLANE[r]), z), plane.at[r]).start()
     plane_all = to(plane.at[pl.ds(1, 15)], plane_sem, (partner, z))
+
+    @pl.when(core == 0)
+    def _():
+        pair_copy.start()
+
+    @pl.when(core == 1)
+    def _():
+        pair_copy.wait_recv()
+        plane[0] = pair[0] + pair[1]
+        for r in range(1, 16):
+            to(plane.at[0], plane_sem, (pts_at(*PLANE[r]), z), plane.at[r]).start()
 
     weights_3(0)
     own = pl.multiple_of(z * OWN, 128)
@@ -274,27 +280,32 @@
     weights_far(0)
 
     qkv_copy.wait()
-    plane_all.wait_recv()
-    sums = jnp.sum(plane[...], axis=0)
-    packed = sums[0:half_g]
-    numerator = jnp.concatenate([packed, pltpu.roll(packed, DH, axis=1)], axis=0)[:, 0:DH]
-    mass = jnp.sum(jnp.where(diagonal, sums[half_g : half_g + 1], 0.0), axis=1, keepdims=True)
-    tokens = numerator / (mass + 1e-05)
-    maps = jnp.concatenate([qkv_ref[0], qkv_ref[1], qkv_ref[2], qkv_ref[2]], axis=1)
-    mapped = jnp.dot(tokens, maps, preferred_element_type=F32, precision=HIGH)
-    scores = contract_lanes(mapped[:, 0:DH], mapped[:, DH : 2 * DH], precision=HIGH) * 0.125
-    values = jnp.where((lane < DH) == (lax.rem(z, 2) == 0), mapped[:, 2 * DH : 4 * DH], 0.0)
-    e = jnp.exp(scores - jnp.max(scores, axis=1, keepdims=True))
-    attend = e / jnp.sum(e, axis=1, keepdims=True)
-    zbuf[z] = jnp.dot(attend, values, preferred_element_type=F32, precision=HIGH).astype(BF16)
-
-    for dz in range(1, H):
-        to(zbuf.at[z], z_sem, (pts, z_at(dz))).start()
-    z_all = to(zbuf.at[pl.ds(0, H - 1)], z_sem, (partner, z))
-
-    weights_far(1)
+
+    @pl.when(core == 1)
+    def _():
+        plane_all.wait_recv()
+        sums = jnp.sum(plane[...], axis=0)
+        packed = sums[0:half_g]
+        numerator = jnp.concatenate([packed, pltpu.roll(packed, DH, axis=1)], axis=0)[:, 0:DH]
+        mass = jnp.sum(jnp.where(diagonal, sums[half_g : half_g + 1], 0.0), axis=1, keepdims=True)
+        tokens = numerator / (mass + 1e-05)
+        maps = jnp.concatenate([qkv_ref[0], qkv_ref[1], qkv_ref[2], qkv_ref[2]], axis=1)
+        mapped = jnp.dot(tokens, maps, preferred_element_type=F32, precision=HIGH)
+        scores = contract_lanes(mapped[:, 0:DH], mapped[:, DH : 2 * DH], precision=HIGH) * 0.125
+        values = jnp.where((lane < DH) == (lax.rem(z, 2) == 0), mapped[:, 2 * DH : 4 * DH], 0.0)
+        e = jnp.exp(scores - jnp.max(scores, axis=1, keepdims=True))
+        attend = e / jnp.sum(e, axis=1, keepdims=True)
+        zbuf[z] = jnp.dot(attend, values, preferred_element_type=F32, precision=HIGH).astype(BF16)
+
+        for dz in range(1, H):
+            to(zbuf.at[z], z_sem, (pts, z_at(dz))).start()
+
+    def z_of(n):
+        return to(zbuf.at[pl.ds(0, n)], z_sem, (partner, z))
+
     weights_done(0)
     yall[...] = contract_lanes(wall[0].reshape(D, D), nown[...]).astype(BF16)
+    weights_far(1)
     for h in range(H):
         if h == 2:
             weights_far(2)
@@ -303,7 +314,15 @@
         logits = jnp.dot(pT[0 : G + 16, 0:DH], yall[h * DH : (h + 1) * DH, :], preferred_element_type=F32)
         wT[h * G : (h + 1) * G, :] = softmax_weights(logits)
     wn[...] = wT[...].T
-    z_all.wait_recv()
+    @pl.when(core == 1)
+    def _():
+        z_of(H - 1).wait_recv()
+        to(zbuf, z_sem, (partner, z)).start()
+
+    @pl.when(core == 0)
+    def _():
+        z_of(H).wait_recv()
+
     weights_done(1)
 
     gap = jnp.zeros((2 * G, 128), BF16)
@@ -344,9 +363,16 @@
         of_size(g, 2, hop_sem).wait_send()
         of_size(g, 3, far_sem).wait_send()
         of_size(g, 7, d2d_sem).wait_send()
-    pair_copy.wait_send()
-    plane_all.wait_send()
-    z_all.wait_send()
+
+    @pl.when(core == 0)
+    def _():
+        pair_copy.wait_send()
+
+    @pl.when(core == 1)
+    def _():
+        plane_all.wait_send()
+        z_of(H).wait_send()
+        z_of(H - 1).wait_send()
 
 
 OUT = pltpu.VMEM((OWN, D), BF16)

time: 33.1 us -> 32.6 us (0.985)
  Pallas kernels: 31.9 us -> 31.4 us
    pallas_call x1, Pallas kernels: 31.9 us -> 31.4 us  [local(): pl.pallas_call(kernel, out_shape=OUT, in_specs=[hbm] * 8, out_specs=vmem,...]
where the time goes in v7:
time: 32.6 us
  Pallas kernels  31.4 us (96%)
  local copies, waits for them, and re-layouts  1.1 us (3%)
    pallas_call x1, Pallas kernels, local(): pl.pallas_call(kernel, out_shape=OUT, in_specs=[hbm] * 8, out_specs=vmem,...  31.4 us
    unnamed x1, local copies, waits for them, and re-layouts  1.1 us

profile of v7, /device:TPU:1, one launch (start us, length us, event | category | flops | bytes accessed | tf_op | source)
XLA Modules:
  0.0 32.6 jit_solution(5989523061620459586)
XLA Ops:
  0.0 31.4 %shard_map.82 = bf16[1408,512]{1,0:T(8,128)(2,1)S(1)} custom-call(bf16[11264,512]{1,0:T(8,128)(2,1)} %x_hbm.1, bf16[64,512]{1,0:T(8,128)(2,1)} %bitcast.3, bf16[32,64]{1,0:T(8,128)(2,1)} %bitcast.4, f32[1,64]{1,0:T(1,128)} %bitcast.5, f32[3,64,64]{2,1,0:T(8,128)} %qkv_hbm.1, bf16[64,512]{1,0:T(8,128)(2,1)} %exit_hbm.1, bf16[64,512]{1,0:T(8,128)(2,1)} %wide_hbm.1, ...), custom_call_target="tpu_custom_call" | custom-call | tf_op jit(solution)/shard_map/pallas_call | solution.py:385
  31.5 1.1 %copy.10 = bf16[1408,512]{1,0:T(8,128)(2,1)} copy(bf16[1408,512]{1,0:T(8,128)(2,1)S(1)} %shard_map.82) | data formatting | bytes 2883584

commit v8 on v7

--- a/solution.py
+++ b/solution.py
@@ -118,48 +118,73 @@
         waug[half * D : (half + 1) * D, 0:128] = jnp.where(lanes, both, 0.0).astype(BF16)
         waug[half * D : (half + 1) * D, 128:256] = jnp.where(lanes, 1.0 / D, 0.0).astype(BF16)
 
+    carrier = {0: 1, 1: 0, 2: 1, 3: 0}
+
     def to(ref, sems, device, target=None):
         return pltpu.make_async_remote_copy(
             src_ref=ref, dst_ref=ref if target is None else target, send_sem=sems.at[0], recv_sem=sems.at[1],
             device_id=device, device_id_type=MESH,
         )
 
-    def half_of(g, offset, half, rows=pl.ds(0, HALF)):
-        return wall.at[g, z_at(offset), half, rows]
+    def by_carrier(g, act, other=False):
+        if g in carrier:
+            pl.when(core == (1 - carrier[g] if other else carrier[g]))(act)
+        else:
+            act()
+
+    def piece(g, offset, side=None):
+        shard = z_at(offset)
+        if g in carrier:
+            return wall.at[g, shard] if side is None else wall.at[g, shard, side]
+        rows = pl.ds(0, HALF) if side is None else pl.ds(side * (HALF // 2), HALF // 2)
+        return wall.at[g, shard, core, rows]
 
     def of_size(g, n, sems):
-        return to(wall.at[g, pl.ds(0, n), 0], sems.at[g], (partner, z))
+        some = wall.at[g, pl.ds(0, n)] if g in carrier else wall.at[g, pl.ds(0, n), 0]
+        return to(some, sems.at[g], (partner, z))
 
     def to_partner(g, offsets):
         for offset in offsets:
-            to(half_of(g, offset, core), d2d_sem.at[g], (partner, z)).start()
+            to(piece(g, offset), d2d_sem.at[g], (partner, z)).start()
 
     def weights_1():
         for copy in own_copies:
             copy.wait()
         for g in range(4):
+
+            def act(g=g):
+                for d in (1, -1):
+                    to(piece(g, 0), own_sem.at[g], (pts, z_at(d))).start()
+
+            by_carrier(g, act)
+
+    def weights_2(g):
+        def act():
+            of_size(g, 2, own_sem).wait_recv()
             for d in (1, -1):
-                to(half_of(g, 0, core), own_sem.at[g], (pts, z_at(d))).start()
-
-    def weights_2(g):
-        of_size(g, 2, own_sem).wait_recv()
-        for d in (1, -1):
-            to(half_of(g, -d, core), hop_sem.at[g], (pts, z_at(d))).start()
+                to(piece(g, -d), hop_sem.at[g], (pts, z_at(d))).start()
+
+        by_carrier(g, act)
 
     def weights_3(g):
-        of_size(g, 2, hop_sem).wait_recv()
-        for d, first in ((1, 0), (-1, HALF // 2)):
-            to(half_of(g, -2 * d, core), far_sem.at[g], (pts, z_at(d))).start()
-            rows = pl.ds(first, HALF // 2)
-            to(half_of(g, -2 * d, core, rows), far_sem.at[g], (pts, z_at(2 * d))).start()
-        to_partner(g, (1, -1, 2, -2))
+        def act():
+            of_size(g, 2, hop_sem).wait_recv()
+            for d, side in ((1, 0), (-1, 1)):
+                to(piece(g, -2 * d), far_sem.at[g], (pts, z_at(d))).start()
+                to(piece(g, -2 * d, side), far_sem.at[g], (pts, z_at(2 * d))).start()
+            to_partner(g, (1, -1, 2, -2))
+
+        by_carrier(g, act)
 
     def weights_far(g):
-        of_size(g, 3, far_sem).wait_recv()
-        to_partner(g, (3, -3, 4))
+        def act():
+            of_size(g, 3, far_sem).wait_recv()
+            to_partner(g, (3, -3, 4))
+
+        by_carrier(g, act)
 
     def weights_done(g):
-        of_size(g, 7, d2d_sem).wait_recv()
+        by_carrier(g, lambda: of_size(g, 7, d2d_sem).wait_recv(), other=True)
 
     def project(i, q, fbuf):
         start = i * BLK + q * DOT
@@ -277,7 +302,6 @@
     lax.fori_loop(0, OWN // NORM_ROWS, own_norm, 0)
     for g in range(1, 4):
         weights_3(g)
-    weights_far(0)
 
     qkv_copy.wait()
 
@@ -303,6 +327,7 @@
     def z_of(n):
         return to(zbuf.at[pl.ds(0, n)], z_sem, (partner, z))
 
+    weights_far(0)
     weights_done(0)
     yall[...] = contract_lanes(wall[0].reshape(D, D), nown[...]).astype(BF16)
     weights_far(1)
@@ -359,10 +384,14 @@
         feed(t, *stage[t % 2])
 
     for g in range(4):
-        of_size(g, 2, own_sem).wait_send()
-        of_size(g, 2, hop_sem).wait_send()
-        of_size(g, 3, far_sem).wait_send()
-        of_size(g, 7, d2d_sem).wait_send()
+
+        def sent(g=g):
+            of_size(g, 2, own_sem).wait_send()
+            of_size(g, 2, hop_sem).wait_send()
+            of_size(g, 3, far_sem).wait_send()
+            of_size(g, 7, d2d_sem).wait_send()
+
+        by_carrier(g, sent)
 
     @pl.when(core == 0)
     def _():

time: 32.6 us -> 32.2 us (0.988)
  Pallas kernels: 31.4 us -> 31 us
    pallas_call x1, Pallas kernels: 31.4 us -> 31 us  [local(): pl.pallas_call(kernel, out_shape=OUT, in_specs=[hbm] * 8, out_specs=vmem,...]
where the time goes in v8:
time: 32.2 us; the launch traced here: 32.1 us
  Pallas kernels  31 us (96%)
  local copies, waits for them, and re-layouts  1.1 us (3%)
    pallas_call x1, Pallas kernels, local(): pl.pallas_call(kernel, out_shape=OUT, in_specs=[hbm] * 8, out_specs=vmem,...  31 us
    unnamed x1, local copies, waits for them, and re-layouts  1.1 us

profile of v8, /device:TPU:1, one launch (start us, length us, event | category | flops | bytes accessed | tf_op | source)
XLA Modules:
  0.0 32.1 jit_solution(1779069106137965831)
XLA Ops:
  0.0 31.0 %shard_map.82 = bf16[1408,512]{1,0:T(8,128)(2,1)S(1)} custom-call(bf16[11264,512]{1,0:T(8,128)(2,1)} %x_hbm.1, bf16[64,512]{1,0:T(8,128)(2,1)} %bitcast.3, bf16[32,64]{1,0:T(8,128)(2,1)} %bitcast.4, f32[1,64]{1,0:T(1,128)} %bitcast.5, f32[3,64,64]{2,1,0:T(8,128)} %qkv_hbm.1, bf16[64,512]{1,0:T(8,128)(2,1)} %exit_hbm.1, bf16[64,512]{1,0:T(8,128)(2,1)} %wide_hbm.1, ...), custom_call_target="tpu_custom_call" | custom-call | tf_op jit(solution)/shard_map/pallas_call | solution.py:414
  31.0 1.1 %copy.10 = bf16[1408,512]{1,0:T(8,128)(2,1)} copy(bf16[1408,512]{1,0:T(8,128)(2,1)S(1)} %shard_map.82) | data formatting | bytes 2883584

commit v9 on v8

--- a/solution.py
+++ b/solution.py
@@ -243,7 +243,7 @@
         for _ in project(0, q, f0):
             pass
 
-    start_at = (z < 1).astype(jnp.int32) + (z < 4).astype(jnp.int32)
+    start_at = (z < 1).astype(jnp.int32) + (z < 3).astype(jnp.int32)
 
     def two_blocks(j, _):
         @pl.when(j == start_at)

time: 32.2 us -> 32.1 us (level)
  no operation moved by 1% of the time
where the time goes in v9:
time: 32.1 us; the launch traced here: 32 us
  Pallas kernels  30.9 us (96%)
  local copies, waits for them, and re-layouts  1.1 us (3%)
    pallas_call x1, Pallas kernels, local(): pl.pallas_call(kernel, out_shape=OUT, in_specs=[hbm] * 8, out_specs=vmem,...  30.9 us
    unnamed x1, local copies, waits for them, and re-layouts  1.1 us

profile of v9, /device:TPU:1, one launch (start us, length us, event | category | flops | bytes accessed | tf_op | source)
XLA Modules:
  0.0 32.0 jit_solution(5428784187815657843)
XLA Ops:
  0.0 30.9 %shard_map.82 = bf16[1408,512]{1,0:T(8,128)(2,1)S(1)} custom-call(bf16[11264,512]{1,0:T(8,128)(2,1)} %x_hbm.1, bf16[64,512]{1,0:T(8,128)(2,1)} %bitcast.3, bf16[32,64]{1,0:T(8,128)(2,1)} %bitcast.4, f32[1,64]{1,0:T(1,128)} %bitcast.5, f32[3,64,64]{2,1,0:T(8,128)} %qkv_hbm.1, bf16[64,512]{1,0:T(8,128)(2,1)} %exit_hbm.1, bf16[64,512]{1,0:T(8,128)(2,1)} %wide_hbm.1, ...), custom_call_target="tpu_custom_call" | custom-call | tf_op jit(solution)/shard_map/pallas_call | solution.py:414
  30.9 1.1 %copy.10 = bf16[1408,512]{1,0:T(8,128)(2,1)} copy(bf16[1408,512]{1,0:T(8,128)(2,1)S(1)} %shard_map.82) | data formatting | bytes 2883584
